TPU v7x, 8 devices: a whole 2x2x1 slice. The times are simulated.
8 devices in a mesh: dp: 1 (over z), ty: 2 (over y), tx: 4 (over x, core).
Axes of the slice: x: 2, y: 2, z: 1, core: 2. Of those that a mesh axis runs over, the one named last changes fastest.
Arguments:
- x_in: bfloat16 [128, 4096], P('dp', 'tx')
- seq_lens: int32 [128], P('dp')
- k_cache: bfloat16 [128, 4096, 128], P(('dp', 'ty', 'tx'))
- v_cache: bfloat16 [128, 4096, 128], P(('dp', 'ty', 'tx'))
- ln_gamma: float32 [4096], P('tx')
- w_query: bfloat16 [4096, 4096], P('tx', 'ty')
- w_key: bfloat16 [4096, 128], P('tx')
- w_value: bfloat16 [4096, 128], P('tx')
- w_gate: bfloat16 [4096, 16384], P('tx', 'ty')
- w_up: bfloat16 [4096, 16384], P('tx', 'ty')
- w_out: bfloat16 [4096, 4096], P('ty', 'tx')
- w_down: bfloat16 [16384, 4096], P('ty', 'tx')
Outputs:
- output 1: bfloat16 [128, 4096], P('dp', 'tx')
- output 2: bfloat16 [128, 4096, 128], P(('dp', 'ty', 'tx'))
- output 3: bfloat16 [128, 4096, 128], P(('dp', 'ty', 'tx'))
All inputs are finite; a program needn't handle non-finite values.
Results may differ from a plain program's by a relative error of at most 0.0135093.
Values are sent between devices in bfloat16 or wider.
A program may use at most 1 GiB of HBM per device.

v0:
```python
import jax
import jax.numpy as jnp
from jax import lax
from jax.sharding import PartitionSpec as P

EPSILON = 1e-6
ROPE_BASE = 10000.0


def rope_tables(positions, head_dim):
    half_dim = head_dim // 2
    inv_freqs = ROPE_BASE ** (-(jnp.arange(half_dim, dtype=jnp.float32) * 2.0) / head_dim)
    angles = positions.astype(jnp.float32)[:, None] * inv_freqs[None, :]
    return jnp.cos(angles), jnp.sin(angles)


def rope_apply(vals, cosines, sines):
    half_dim = vals.shape[-1] // 2
    first = vals[..., :half_dim]
    second = vals[..., half_dim:]
    return jnp.concatenate([first * cosines - second * sines, second * cosines + first * sines], axis=-1)


def solution(mesh):
    ty_size = mesh.shape["ty"]
    tx_size = mesh.shape["tx"]
    cache_spec = P(("dp", "ty", "tx"), None, None)

    def layer_shard(x_blk, lens_part, k_blk, v_blk, gamma_blk, w_query, w_key, w_value, w_gate, w_up, w_out, w_down):
        rows = x_blk.shape[0]
        d_model = x_blk.shape[1] * tx_size
        seq_block, ctx_len, head_dim = k_blk.shape
        local_heads = w_query.shape[1] // head_dim
        row_idx = lax.axis_index("ty")
        col_idx = lax.axis_index("tx")

        x_f32 = x_blk.astype(jnp.float32)
        row_stats = jnp.stack([jnp.sum(x_f32, axis=-1), jnp.sum(x_f32 * x_f32, axis=-1)], axis=-1)
        row_stats = lax.psum(row_stats, "tx")
        row_mean = row_stats[:, 0] / d_model
        row_var = row_stats[:, 1] / d_model - row_mean * row_mean
        normed = ((x_f32 - row_mean[:, None]) * lax.rsqrt(row_var[:, None] + EPSILON) * gamma_blk[None, :]).astype(jnp.bfloat16)

        partials = tuple(jnp.dot(normed, weight, preferred_element_type=jnp.float32).astype(jnp.bfloat16) for weight in (w_query, w_key, w_value, w_gate, w_up))
        q_sum, k_sum, v_new, gate, up_proj = lax.psum(partials, "tx")

        cosines, sines = rope_tables(lens_part, head_dim)
        queries = rope_apply(q_sum.astype(jnp.float32).reshape(rows, local_heads, head_dim), cosines[:, None, :], sines[:, None, :]).astype(jnp.bfloat16)
        k_new = rope_apply(k_sum.astype(jnp.float32), cosines, sines).astype(jnp.bfloat16)

        block_start = (row_idx * tx_size + col_idx) * seq_block
        lens_own = lax.dynamic_slice_in_dim(lens_part, block_start, seq_block)
        k_own = lax.dynamic_slice_in_dim(k_new, block_start, seq_block)
        v_own = lax.dynamic_slice_in_dim(v_new, block_start, seq_block)
        positions = jnp.arange(ctx_len)
        at_slot = positions[None, :, None] == lens_own[:, None, None]
        k_out = jnp.where(at_slot, k_own[:, None, :], k_blk)
        v_out = jnp.where(at_slot, v_own[:, None, :], v_blk)

        q_column = lax.dynamic_index_in_dim(queries.reshape(ty_size, tx_size, seq_block, local_heads, head_dim), col_idx, axis=1, keepdims=False)
        q_owned = lax.all_to_all(q_column, "ty", 0, 0, tiled=True)
        scores = jnp.einsum("gbhd,btd->gbht", q_owned, k_out, preferred_element_type=jnp.float32) * (head_dim ** -0.5)
        in_range = positions[None, None, None, :] <= lens_own[None, :, None, None]
        scores = jnp.where(in_range, scores, -1e30)
        att_probs = jax.nn.softmax(scores, axis=-1).astype(jnp.bfloat16)
        att_owned = jnp.einsum("gbht,btd->gbhd", att_probs, v_out, preferred_element_type=jnp.float32).astype(jnp.bfloat16)
        att_column = lax.all_to_all(att_owned, "ty", 0, 0, tiled=True)
        att_rows = lax.all_gather(att_column, "tx", axis=1, tiled=False).reshape(rows, local_heads * head_dim)

        mlp_act = (jax.nn.silu(gate.astype(jnp.float32)) * up_proj.astype(jnp.float32)).astype(jnp.bfloat16)
        part_out = jnp.dot(att_rows, w_out, preferred_element_type=jnp.float32) + jnp.dot(mlp_act, w_down, preferred_element_type=jnp.float32)
        out_sum = lax.psum(part_out.astype(jnp.bfloat16), "ty")
        y_blk = (x_f32 + out_sum.astype(jnp.float32)).astype(jnp.bfloat16)
        return y_blk, k_out, v_out

    in_specs = (P("dp", "tx"), P("dp"), cache_spec, cache_spec, P("tx"), P("tx", "ty"), P("tx", None), P("tx", None), P("tx", "ty"), P("tx", "ty"), P("ty", "tx"), P("ty", "tx"))
    out_specs = (P("dp", "tx"), cache_spec, cache_spec)
    return jax.shard_map(layer_shard, mesh=mesh, in_specs=in_specs, out_specs=out_specs, check_vma=False)
```

profile of v0, /device:TPU:0, one launch (start us, length us, event | category | flops | bytes accessed | tf_op | source)
XLA Modules:
  0.0 245.9 jit_solution(3743672885680056659)
XLA Ops:
  7.2 0.0 copy-start
  7.2 0.0 all-reduce.8.cloned.1.call-start
  7.2 1.1 convert_reduce_fusion
  8.4 8.8 %psum.49 = f32[128,2]{0,1:T(2,128)S(1)} all-reduce(f32[128,2]{0,1:T(2,128)S(1)} %pad_maximum_fusion), channel_id=1, replica_groups=mesh['dp'=1,'ty'=2,'tx'=4] {'tx'}, use_global_device_ids=true, to_apply=%region_2.0 | all-reduce | flops 256 | bytes 2048 | tf_op jit(solution)/shard_map/psum | solution.py:39
  17.1 0.0 copy-done
  17.1 1.9 convolution_convert_fusion.3
  19.0 1.9 convolution_convert_fusion.4
  20.9 0.0 all-reduce.8.cloned.1.call-update
  21.0 0.0 copy-start.3
  21.0 0.0 copy-start.5
  21.0 0.0 all-reduce.10.cloned.1.call-start
  21.0 0.0 copy-start.2
  21.1 9.8 %convolution_convert_fusion.1 = bf16[128,8192]{1,0:T(8,128)(2,1)} fusion(bf16[1024,8192]{1,0:T(8,128)(2,1)} %param.20, bf16[128,1024]{1,0:T(8,128)(2,1)} %param.12, f32[1024]{0:T(1024)} %param.16, f32[128]{0:T(128)S(1)} %get-tuple-element.21, f32[128]{0:T(128)S(1)} %get-tuple-element.20), kind=kOutput, calls=%fused_computation.8 | convolution fusion | flops 2149187584 | bytes 19141632 | tf_op jit(solution)/shard_map/dot_general | solution.py:44
  30.8 0.0 copy-done.3
  30.8 0.0 copy-done.5
  30.8 1.7 copy-done.2
  32.5 3.8 %convolution_convert_fusion = bf16[128,8192]{1,0:T(8,128)(2,1)} fusion(bf16[1024,8192]{1,0:T(8,128)(2,1)S(1)} %copy-done.2, bf16[128,1024]{1,0:T(8,128)(2,1)S(1)} %copy-done.3, f32[1024]{0:T(1024)S(1)} %copy-done.5, f32[128]{0:T(128)S(1)} %get-tuple-element.21, f32[128]{0:T(128)S(1)} %get-tuple-element.20), kind=kOutput, calls=%fused_computation.7 | convolution fusion | flops 2149187584 | bytes 19141632 | tf_op jit(solution)/shard_map/dot_general | solution.py:44
  36.3 0.8 fusion.21
  37.1 0.9 copy.30
  38.0 0.0 all-reduce.10.cloned.1.call-update
  38.1 0.1 dynamic_slice.13
  38.1 0.1 iota_compare_fusion
  38.3 8.9 %all-reduce.8.cloned.1.call-done = (bf16[128,128]{1,0:T(8,128)(2,1)}, bf16[128,128]{1,0:T(8,128)(2,1)}) async-done(((bf16[128,128]{1,0:T(8,128)(2,1)}, bf16[128,128]{1,0:T(8,128)(2,1)}), (bf16[128,128]{1,0:T(8,128)(2,1)}, bf16[128,128]{1,0:T(8,128)(2,1)})) %all-reduce.8.cloned.1.call-update) | async-done | bytes 65552 | tf_op jit(solution)/shard_map/psum | solution.py:45
  47.2 0.8 convert_element_type.62
  47.9 0.3 multiply_cosine_fusion
  48.2 0.8 fusion.39
  49.0 89.6 %all-reduce.10.cloned.1.call-done = (bf16[128,8192]{1,0:T(8,128)(2,1)}, bf16[128,8192]{1,0:T(8,128)(2,1)}, bf16[128,16,128]{2,1,0:T(8,128)(2,1)}) async-done(((bf16[128,8192]{1,0:T(8,128)(2,1)}, bf16[128,8192]{1,0:T(8,128)(2,1)}, bf16[128,16,128]{2,1,0:T(8,128)(2,1)}), (bf16[128,8192]{1,0:T(8,128)(2,1)}, bf16[128,8192]{1,0:T(8,128)(2,1)}, bf16[128,16,128]{2,1,0:T(8,128)(2,1)})) %all-reduce.10.cloned.1.call-update) | async-done | bytes 4718608 | tf_op jit(solution)/shard_map/psum | solution.py:45
  138.6 1.1 reshape.126
  139.7 0.5 add_convert_fusion
  140.3 0.8 fusion.37
  141.0 3.6 %all-to-all-start = ((bf16[2,16,16,128]{3,2,1,0:T(8,128)(2,1)}), bf16[2,16,16,128]{3,2,1,0:T(8,128)(2,1)S(1)}, u32[]{:S(2)}, u32[]{:S(2)}) async-start(bf16[2,16,16,128]{3,2,1,0:T(8,128)(2,1)} %fusion.37), calls=%async_computation | async-start | bytes 262144 | tf_op jit(solution)/shard_map/all_to_all | solution.py:61
  144.6 23.3 %broadcast_select_fusion.1 = (bf16[16,4096,128]{2,1,0:T(8,128)(2,1)}, bf16[16,4096,128]{2,1,0:T(8,128)(2,1)}) fusion(bf16[16,4096,128]{2,1,0:T(8,128)(2,1)} %param.15, pred[16,4096]{1,0:T(8,128)(4,1)S(1)} %get-tuple-element.23, bf16[16,128]{1,0:T(8,128)(2,1)S(1)} %get-tuple-element.27, bf16[16,4096,128]{2,1,0:T(8,128)(2,1)} %param.14, ...), kind=kLoop, calls=%fused_computation.6 | loop fusion | flops 16777216 | bytes 67182592 | tf_op jit(solution)/shard_map/jit(_where)/select_n | solution.py:58
  167.9 0.0 all-to-all-done
  167.9 9.3 %fusion.1 = f32[16,4096,2,16]{1,3,2,0:T(8,128)S(1)} fusion(bf16[16,4096,128]{2,1,0:T(8,128)(2,1)} %get-tuple-element.15, bf16[2,16,16,128]{3,2,1,0:T(8,128)(2,1)S(1)} %all-to-all-done), kind=kOutput, calls=%fused_computation.1 | convolution fusion | flops 536870912 | bytes 25296896 | tf_op jit(solution)/shard_map/gbhd,btd->gbht/dot_general | solution.py:62
  177.3 5.5 %fusion.49 = (f32[2,16,16]{2,0,1:T(2,128)S(1)}, f32[2,16,16,4096]{3,2,0,1:T(8,128)}) fusion(f32[16,4096,2,16]{1,3,2,0:T(8,128)S(1)} %fusion.1, pred[16,4096]{1,0:T(8,128)(4,1)S(1)} %get-tuple-element.22), kind=kOutput, calls=%fused_computation.72 | output fusion | flops 12587007 | bytes 16844800 | tf_op jit(solution)/shard_map/sub | solution.py:65
  182.7 9.7 %fusion.26 = bf16[2,16,16,128]{3,2,0,1:T(8,128)(2,1)S(1)} fusion(f32[2,16,16,4096]{3,2,0,1:T(8,128)} %get-tuple-element.25, f32[2,16,16]{2,0,1:T(2,128)S(1)} %get-tuple-element.24, bf16[16,4096,128]{2,1,0:T(8,128)(2,1)} %get-tuple-element.14), kind=kOutput, calls=%fused_computation.33 | convolution fusion | flops 541130752 | bytes 25298944 | tf_op jit(solution)/shard_map/gbht,btd->gbhd/dot_general | solution.py:66
  192.4 0.7 copy.23
  193.1 3.4 %all-to-all-start.1 = ((bf16[2,16,16,128]{3,2,1,0:T(8,128)(2,1)}), bf16[2,16,16,128]{3,2,1,0:T(8,128)(2,1)S(1)}, u32[]{:S(2)}, u32[]{:S(2)}) async-start(bf16[2,16,16,128]{3,2,1,0:T(8,128)(2,1)} %copy.23), calls=%async_computation.1 | async-start | bytes 262144 | tf_op jit(solution)/shard_map/all_to_all | solution.py:67
  196.5 0.0 all-reduce.6.cloned.1.call-start
  196.5 0.0 copy-done.6
  196.6 0.0 copy-start.1
  196.6 9.3 %fusion.18 = f32[128,1024]{1,0:T(8,128)S(1)} fusion(bf16[8192,1024]{1,0:T(8,128)(2,1)} %param.23, bf16[128,8192]{1,0:T(8,128)(2,1)S(1)} %copy-done.6, bf16[128,8192]{1,0:T(8,128)(2,1)} %get-tuple-element.8), kind=kOutput, calls=%fused_computation.27 | convolution fusion | flops 2155872256 | bytes 21495808 | tf_op jit(solution)/shard_map/dot_general | solution.py:71
  205.8 0.0 all-to-all-done.1
  205.9 9.0 %all-gather = bf16[2,64,16,128]{3,2,0,1:T(8,128)(2,1)S(1)} all-gather(bf16[2,16,16,128]{3,2,0,1:T(8,128)(2,1)S(1)} %copy.24), channel_id=2, replica_groups=mesh['dp'=1,'ty'=2,'tx'=4] {'tx'}, dimensions={1}, use_global_device_ids=true | all-gather | bytes 655360 | tf_op jit(solution)/shard_map/all_gather | solution.py:68
  214.9 3.6 %fusion.22 = bf16[128,1024]{1,0:T(8,128)(2,1)} fusion(f32[128,1024]{1,0:T(8,128)S(1)} %fusion.18, bf16[2048,1024]{1,0:T(8,128)(2,1)} %param.22, bf16[16,8,16,128]{3,2,1,0:T(8,128)(2,1)S(1)} %bitcast.57), kind=kOutput, calls=%fused_computation.31 | convolution fusion | flops 537133056 | bytes 5505024 | tf_op jit(solution)/shard_map/dot_general | solution.py:71
  218.6 0.0 all-reduce.6.cloned.1.call-update
  218.6 19.1 %all-reduce.6.cloned.1.call-done = bf16[128,1024]{1,0:T(8,128)(2,1)} async-done(((bf16[128,1024]{1,0:T(8,128)(2,1)}), bf16[128,1024]{1,0:T(8,128)(2,1)}) %all-reduce.6.cloned.1.call-update) | async-done | bytes 262160 | tf_op jit(solution)/shard_map/psum | solution.py:72
  237.7 1.7 fusion.33
  (12 shorter events, 0.1 us)
Async XLA Ops:
  7.2 10.0 %copy-start = (bf16[1024,128]{1,0:T(8,128)(2,1)S(1)}, bf16[1024,128]{1,0:T(8,128)(2,1)}, u32[]{:S(2)}) copy-start(bf16[1024,128]{1,0:T(8,128)(2,1)} %param.18) | copy-start | bytes 786436
  7.2 40.0 %all-reduce.8.cloned.1.call-start = ((), (), s32[]{:S(2)}) async-start(), calls=%async_computation.3 | async-start | bytes 131072 | tf_op jit(solution)/shard_map/psum | solution.py:45
  21.0 9.9 %copy-start.3 = (bf16[128,1024]{1,0:T(8,128)(2,1)S(1)}, bf16[128,1024]{1,0:T(8,128)(2,1)}, u32[]{:S(2)}) copy-start(bf16[128,1024]{1,0:T(8,128)(2,1)} %param.12) | copy-start | bytes 786436
  21.0 9.8 %copy-start.5 = (f32[1024]{0:T(1024)S(1)}, f32[1024]{0:T(1024)}, u32[]{:S(2)}) copy-start(f32[1024]{0:T(1024)} %param.16) | copy-start | bytes 12292
  21.0 117.6 %all-reduce.10.cloned.1.call-start = ((), (), s32[]{:S(2)}) async-start(), calls=%async_computation.4 | async-start | bytes 9437184 | tf_op jit(solution)/shard_map/psum | solution.py:45
  21.0 11.4 %copy-start.2 = (bf16[1024,8192]{1,0:T(8,128)(2,1)S(1)}, bf16[1024,8192]{1,0:T(8,128)(2,1)}, u32[]{:S(2)}) copy-start(bf16[1024,8192]{1,0:T(8,128)(2,1)} %param.21) | copy-start | bytes 50331652
  32.5 3.8 %copy-start.4 = (bf16[1024,2048]{1,0:T(8,128)(2,1)S(1)}, bf16[1024,2048]{1,0:T(8,128)(2,1)}, u32[]{:S(2)}) copy-start(bf16[1024,2048]{1,0:T(8,128)(2,1)} %param.17) | copy-start | bytes 12582916
  36.3 1.7 copy-start.7
  141.0 26.9 %all-to-all-start = ((bf16[2,16,16,128]{3,2,1,0:T(8,128)(2,1)}), bf16[2,16,16,128]{3,2,1,0:T(8,128)(2,1)S(1)}, u32[]{:S(2)}, u32[]{:S(2)}) async-start(bf16[2,16,16,128]{3,2,1,0:T(8,128)(2,1)} %fusion.37), calls=%async_computation | async-start | bytes 262144 | tf_op jit(solution)/shard_map/all_to_all | solution.py:61
  182.7 13.8 %copy-start.6 = (bf16[128,8192]{1,0:T(8,128)(2,1)S(1)}, bf16[128,8192]{1,0:T(8,128)(2,1)}, u32[]{:S(2)}) copy-start(bf16[128,8192]{1,0:T(8,128)(2,1)} %get-tuple-element.7) | copy-start | bytes 6291460
  193.1 12.7 %all-to-all-start.1 = ((bf16[2,16,16,128]{3,2,1,0:T(8,128)(2,1)}), bf16[2,16,16,128]{3,2,1,0:T(8,128)(2,1)S(1)}, u32[]{:S(2)}, u32[]{:S(2)}) async-start(bf16[2,16,16,128]{3,2,1,0:T(8,128)(2,1)} %copy.23), calls=%async_computation.1 | async-start | bytes 262144 | tf_op jit(solution)/shard_map/all_to_all | solution.py:67
  196.5 41.2 %all-reduce.6.cloned.1.call-start = ((), (), s32[]{:S(2)}) async-start(), calls=%async_computation.2 | async-start | bytes 524288 | tf_op jit(solution)/shard_map/psum | solution.py:72
  196.6 42.8 %copy-start.1 = (bf16[1024,128]{1,0:T(8,128)(2,1)S(1)}, bf16[1024,128]{1,0:T(8,128)(2,1)}, u32[]{:S(2)}) copy-start(bf16[1024,128]{1,0:T(8,128)(2,1)} %param.18) | copy-start | bytes 786436
Sparse Core Ops, SparseCore 0:
  21.1 26.0 all-reduce.7
  50.3 88.2 all-reduce.9
  218.7 18.9 all-reduce.5
where the time goes:
time: 246 us
  waiting for transfers between devices  118 us (48%)
  matrix products  50.1 us (20%)
  other arithmetic  36.1 us (15%)
  blocking collectives  17.8 us (7%)
  between operations  13.9 us (6%)
  starting transfers between devices  7.06 us (3%)
  local copies, waits for them, and re-layouts  3.37 us (1%)
    psum x2, waiting for transfers between devices, layer_shard(): q_sum, k_sum, v_new, gate, up_proj = lax.psum(partials, 'tx')  98.4 us
    select_n x1, other arithmetic, layer_shard(): v_out = jnp.where(at_slot, v_own[:, None, :], v_blk)  23.3 us
    psum x1, waiting for transfers between devices, layer_shard(): out_sum = lax.psum(part_out.astype(jnp.bfloat16), 'ty')  19.1 us
    dot_general x5, matrix products, layer_shard(): jnp.dot(normed, weight, preferred_element_type=jnp.float32)  18.2 us
    dot_general x1, matrix products, layer_shard(): jnp.einsum('gbht,btd->gbhd', att_probs, v_out, preferred_element_type=jnp...  9.72 us
    dot_general x1, matrix products, layer_shard(): jnp.einsum('gbhd,btd->gbht', q_owned, k_out, preferred_element_type=jnp.f...  9.33 us
    dot_general x1, matrix products, layer_shard(): jnp.dot(mlp_act, w_down, preferred_element_type=jnp.float32)  9.26 us
    all_gather x1, blocking collectives, layer_shard(): lax.all_gather(att_column, 'tx', axis=1, tiled=False)  9.04 us
  transfers between devices with their start and end apart: 5, of which 3 were waited for; matrix products, arithmetic and copies ran while one was open for 20% of the time, Pallas kernels for 0%

commit v1 on v0

v1 whole, which is shorter than its diff:
```python
import functools

import jax
import jax.numpy as jnp
from jax import lax
from jax.experimental import pallas as pl
from jax.experimental.pallas import tpu as pltpu
from jax.sharding import PartitionSpec as P

EPSILON = 1e-6
ROPE_BASE = 10000.0
BF16 = jnp.bfloat16
F32 = jnp.float32
MESH = pl.DeviceIdType.MESH

VMEM = pltpu.VMEM
DMA = pltpu.SemaphoreType.DMA


def here():
    row = lax.axis_index("ty")
    col = lax.axis_index("tx")
    return row, col, col // 2, col % 2


def greet_all():
    row, col, _, _ = here()
    me = row * 4 + col
    barrier = pltpu.get_barrier_semaphore()
    for step in range(1, 8):
        peer = (me + step) % 8
        pl.semaphore_signal(barrier, inc=1, device_id={"ty": peer // 4, "tx": peer % 4}, device_id_type=MESH)
    pl.semaphore_wait(barrier, 7)


def remote(src, dst, send_sem, recv_sem, ty, tx):
    return pltpu.make_async_remote_copy(
        src_ref=src, dst_ref=dst, send_sem=send_sem, recv_sem=recv_sem,
        device_id={"ty": ty, "tx": tx}, device_id_type=MESH)


def dot(a, b):
    return jnp.dot(a, b, preferred_element_type=F32)


def project_kernel(x_ref, gamma_ref, cos_ref, sin_ref, wq_h, wk_h, wv_h, wg_h, wu_h,
                   q_out, kv_out, keep_out, xs_out,
                   wq_v, wkv_v, wg_v, wu_v, h_v, st_send, st_recv,
                   qp, qd, qx, qr, kvp, kvr, qscr, dsend, drecv, own,
                   wq_sem, wkv_sem, w_sem, st_ssem, st_rsem, qd_ssem, qd_rsem, q_ssem, q_rsem,
                   kv_ssem, kv_rsem, d_ssem, d_rsem):
    row, col, chip, core = here()
    partner = col + 1 - 2 * core
    n_chunk = dsend.shape[0]

    wq_cp = [pltpu.make_async_copy(wq_h.at[:, pl.ds(512 * p, 512)], wq_v.at[p], wq_sem.at[p]) for p in range(4)]
    kv_cp = [pltpu.make_async_copy(w.at[:, :], wkv_v.at[:, pl.ds(128 * p, 128)], wkv_sem.at[p]) for p, w in enumerate((wk_h, wv_h))]
    for cp in wq_cp + kv_cp:
        cp.start()

    def weight_copies(n):
        out = []
        for quarter in range(4):
            cols = pl.ds(pl.multiple_of(2048 * quarter + 256 * n, 256), 256)
            out.append(pltpu.make_async_copy(wg_h.at[:, cols], wg_v.at[n, quarter], w_sem.at[n, quarter, 0]))
            out.append(pltpu.make_async_copy(wu_h.at[:, cols], wu_v.at[n, quarter], w_sem.at[n, quarter, 1]))
        return out

    def start_weights(n, carry):
        for cp in weight_copies(n):
            cp.start()
        return carry

    lax.fori_loop(0, n_chunk, start_weights, 0)

    xf = x_ref[...].astype(F32)
    sum1 = jnp.sum(xf, axis=1, keepdims=True)
    sum2 = jnp.sum(xf * xf, axis=1, keepdims=True)
    rows = xf.shape[0]
    eye = lax.broadcasted_iota(jnp.int32, (rows, rows), 0) == lax.broadcasted_iota(jnp.int32, (rows, rows), 1)
    line1 = jnp.sum(jnp.where(eye, sum1, 0.0), axis=0, keepdims=True)
    line2 = jnp.sum(jnp.where(eye, sum2, 0.0), axis=0, keepdims=True)
    first = lax.broadcasted_iota(jnp.int32, (8, rows), 0) == 0
    st_send[...] = jnp.where(first, line1, line2)
    greet_all()
    st_cp = [remote(st_send, st_recv.at[d - 1], st_ssem.at[d - 1], st_rsem.at[d - 1], row, (col + d) % 4) for d in (1, 2, 3)]
    for cp in st_cp:
        cp.start()
    for cp in st_cp:
        cp.wait_recv()
    total = st_send[...] + st_recv[0] + st_recv[1] + st_recv[2]
    width = 4.0 * xf.shape[1]
    mean_line = total[0:1] / width
    var_line = total[1:2] / width - mean_line * mean_line
    rstd_line = lax.rsqrt(var_line + EPSILON)
    mean = jnp.sum(jnp.where(eye, mean_line, 0.0), axis=1, keepdims=True)
    rstd = jnp.sum(jnp.where(eye, rstd_line, 0.0), axis=1, keepdims=True)
    h_v[...] = ((xf - mean) * rstd * gamma_ref[...]).astype(BF16)

    for p in range(4):
        wq_cp[p].wait()
        part = dot(h_v[...], wq_v[p]).astype(BF16)
        for d in range(8):
            qp[d % 2, d // 2, :, 512 * p:512 * p + 512] = part[16 * d:16 * d + 16]
    qd_cp = remote(qp.at[1 - core], qd, qd_ssem, qd_rsem, row, partner)
    qd_cp.start()
    for cp in kv_cp:
        cp.wait()
    kvp[...] = dot(h_v[...], wkv_v[...]).reshape(8, 16, 256)
    kv_sends = []
    for d in (1, 2, 3):
        peer = (col + d) % 4
        cp = remote(kvp.at[row * 4 + peer], kvr.at[d - 1], kv_ssem.at[d - 1], kv_rsem.at[d - 1], row, peer)
        cp.start()
        kv_sends.append(cp)

    def pair_copy(n):
        return remote(dsend.at[n], drecv.at[n], d_ssem.at[n], d_rsem.at[n], row, partner)

    def compute_chunk(n):
        for cp in weight_copies(n):
            cp.wait()
        for xr in range(2):
            quarter = 2 * xr + (1 - core)
            dsend[n, xr, 0] = dot(h_v[...], wg_v[n, quarter]).astype(BF16)
            dsend[n, xr, 1] = dot(h_v[...], wu_v[n, quarter]).astype(BF16)
        pair_copy(n).start()
        for xr in range(2):
            quarter = 2 * xr + core
            own[n % 2, xr, 0] = dot(h_v[...], wg_v[n, quarter])
            own[n % 2, xr, 1] = dot(h_v[...], wu_v[n, quarter])

    def sum_chunk(n):
        pair_copy(n).wait_recv()
        keep_out[:, n] = (own[n % 2, chip] + drecv[n, chip].astype(F32)).astype(BF16)
        xs_out[:, n] = (own[n % 2, 1 - chip] + drecv[n, 1 - chip].astype(F32)).astype(BF16)

    compute_chunk(0)

    qd_cp.wait_recv()
    qx[...] = (qp[core].astype(F32) + qd[...].astype(F32)).astype(BF16)
    mine = row * 2 + chip
    q_sends = []
    for s, (dy, dx) in enumerate(((0, 1), (1, 0), (1, 1))):
        ty, xx = (row + dy) % 2, (chip + dx) % 2
        cp = remote(qx.at[ty * 2 + xx], qr.at[s], q_ssem.at[s], q_rsem.at[s], ty, xx * 2 + core)
        cp.start()
        q_sends.append(cp)

    def step(n, carry):
        compute_chunk(n)
        sum_chunk(n - 1)
        return carry

    lax.fori_loop(1, n_chunk, step, 0)

    me = row * 4 + col
    own_rows = pl.ds(pl.multiple_of(me * 16, 16), 16)
    cosv = cos_ref[own_rows, :]
    sinv = sin_ref[own_rows, :]

    def rotate(vals):
        return vals * cosv + pltpu.roll(vals, 64, 1) * sinv

    for cp in q_sends:
        cp.wait_recv()
    q_same = qx[mine].astype(F32) + qr[0].astype(F32)
    q_diff = qr[1].astype(F32) + qr[2].astype(F32)
    for half, vals in ((row, q_same), (1 - row, q_diff)):
        for head in range(16):
            qscr[half, :, head, :] = rotate(vals[:, 128 * head:128 * head + 128])
    q_out[...] = qscr[...].astype(BF16)
    for cp in kv_sends:
        cp.wait_recv()
    kv = kvp[me] + kvr[0] + kvr[1] + kvr[2]
    kv_out[0] = rotate(kv[:, :128]).astype(BF16).astype(F32)
    kv_out[1] = kv[:, 128:].astype(BF16).astype(F32)

    sum_chunk(n_chunk - 1)
    for cp in st_cp + [qd_cp] + kv_sends + q_sends:
        cp.wait_send()

    def drain(n, carry):
        pair_copy(n).wait_send()
        return carry

    lax.fori_loop(0, n_chunk, drain, 0)


def project(x_blk, gamma, cos2, sin2, w_query, w_key, w_value, w_gate, w_up):
    rows, width = x_blk.shape
    nc = 8
    vm = pl.BlockSpec(memory_space=VMEM)
    hbm = pl.BlockSpec(memory_space=pl.ANY)
    return pl.pallas_call(
        project_kernel,
        out_shape=(
            jax.ShapeDtypeStruct((2, 16, 16, 128), BF16),
            jax.ShapeDtypeStruct((2, 16, 128), F32),
            jax.ShapeDtypeStruct((2, nc, rows, 256), BF16),
            jax.ShapeDtypeStruct((2, nc, rows, 256), BF16),
        ),
        in_specs=[vm] * 4 + [hbm] * 5,
        out_specs=(vm,) * 4,
        scratch_shapes=[
            VMEM((4, width, 512), BF16), VMEM((width, 256), BF16),
            VMEM((nc, 4, width, 256), BF16), VMEM((nc, 4, width, 256), BF16),
            VMEM((rows, width), BF16), VMEM((8, rows), F32), VMEM((3, 8, rows), F32),
            VMEM((2, 4, 16, 2048), BF16), VMEM((4, 16, 2048), BF16), VMEM((4, 16, 2048), BF16), VMEM((3, 16, 2048), BF16),
            VMEM((8, 16, 256), F32), VMEM((3, 16, 256), F32), VMEM((2, 16, 16, 128), F32),
            VMEM((nc, 2, 2, rows, 256), BF16), VMEM((nc, 2, 2, rows, 256), BF16), VMEM((2, 2, 2, rows, 256), F32),
            DMA((4,)), DMA((2,)), DMA((nc, 4, 2)), DMA((3,)), DMA((3,)), DMA, DMA, DMA((3,)), DMA((3,)),
            DMA((3,)), DMA((3,)), DMA((nc,)), DMA((nc,)),
        ],
        compiler_params=pltpu.CompilerParams(collective_id=0, has_side_effects=True, vmem_limit_bytes=56 * 2 ** 20),
        name="project",
    )(x_blk, gamma, cos2, sin2, w_query, w_key, w_value, w_gate, w_up)


SLOTS = 8
AHEAD = 6
BLOCK = 1024
FIRST = 10


def attend_kernel(first, count, lens_ref, q_ref, kv_ref, k_in, v_in, *refs):
    if first:
        refs = refs[2:]
    k_out, v_out, att_out, kbuf, vbuf, s_scr, o_scr, in_sem, out_sem = refs
    row, col, _, _ = here()
    base = (row * 4 + col) * 16
    ctx = k_in.shape[1]

    def in_copies(t):
        slot = lax.rem(t, SLOTS)
        return (pltpu.make_async_copy(k_in.at[first + t], kbuf.at[slot], in_sem.at[slot, 0]),
                pltpu.make_async_copy(v_in.at[first + t], vbuf.at[slot], in_sem.at[slot, 1]))

    def out_copies(t):
        slot = lax.rem(t, SLOTS)
        return (pltpu.make_async_copy(kbuf.at[slot], k_out.at[first + t], out_sem.at[slot, 0]),
                pltpu.make_async_copy(vbuf.at[slot], v_out.at[first + t], out_sem.at[slot, 1]))

    for t in range(min(AHEAD, count)):
        for cp in in_copies(t):
            cp.start()

    def attend(t, slot, length, blocks):
        q = jnp.concatenate([q_ref[0, first + t], q_ref[1, first + t]], axis=0)
        scale = 128.0 ** -0.5
        peak = None
        for b in range(blocks):
            scores = lax.dot_general(q, kbuf[slot, b * BLOCK:(b + 1) * BLOCK, :], (((1,), (1,)), ((), ())),
                                     preferred_element_type=F32) * scale
            if b == blocks - 1:
                pos = lax.broadcasted_iota(jnp.int32, scores.shape, 1) + b * BLOCK
                scores = jnp.where(pos <= length, scores, -1e30)
            s_scr[:, b * BLOCK:(b + 1) * BLOCK] = scores
            for g in range(BLOCK // 128):
                piece = scores[:, g * 128:(g + 1) * 128]
                peak = piece if peak is None else jnp.maximum(peak, piece)
        peak = jnp.max(peak, axis=1, keepdims=True)
        denom = None
        for b in range(blocks):
            e = jnp.exp(s_scr[:, b * BLOCK:(b + 1) * BLOCK] - peak)
            s_scr[:, b * BLOCK:(b + 1) * BLOCK] = e
            for g in range(BLOCK // 128):
                piece = e[:, g * 128:(g + 1) * 128]
                denom = piece if denom is None else denom + piece
        inv = 1.0 / jnp.sum(denom, axis=1, keepdims=True)
        out = None
        for b in range(blocks):
            probs = (s_scr[:, b * BLOCK:(b + 1) * BLOCK] * inv).astype(BF16)
            part = dot(probs, vbuf[slot, b * BLOCK:(b + 1) * BLOCK, :])
            out = part if out is None else out + part
        o_scr[t] = out

    def body(t, carry):
        slot = lax.rem(t, SLOTS)
        for cp in in_copies(t):
            cp.wait()
        length = lens_ref[base + first + t]
        start = pl.multiple_of((length // 16) * 16, 16)
        at_row = lax.broadcasted_iota(jnp.int32, (16, 128), 0) == length - start
        for which, buf in ((0, kbuf), (1, vbuf)):
            old = buf[slot, pl.ds(start, 16), :].astype(F32)
            new = kv_ref[which, pl.ds(first + t, 1), :]
            buf[slot, pl.ds(start, 16), :] = jnp.where(at_row, new, old).astype(BF16)
        for cp in out_copies(t):
            cp.start()

        @pl.when(t + AHEAD < count)
        def _():
            @pl.when(t >= SLOTS - AHEAD)
            def _():
                for cp in out_copies(t - (SLOTS - AHEAD)):
                    cp.wait()

            for cp in in_copies(t + AHEAD):
                cp.start()

        blocks = length // BLOCK
        for b in range(ctx // BLOCK):
            @pl.when(blocks == b)
            def _():
                attend(t, slot, length, b + 1)

        return carry

    lax.fori_loop(0, count, body, 0)

    for head in range(32):
        att_out[head // 16, :, 128 * (head % 16):128 * (head % 16) + 128] = o_scr[:, head, :].astype(BF16)

    done_in_loop = max(0, count - AHEAD - (SLOTS - AHEAD)) if count > AHEAD else 0
    for t in range(done_in_loop, count):
        for cp in out_copies(t):
            cp.wait()


def attend(first, count, lens, q, kv, k_blk, v_blk, prior=()):
    vm = pl.BlockSpec(memory_space=VMEM)
    hbm = pl.BlockSpec(memory_space=pltpu.HBM)
    smem = pl.BlockSpec(memory_space=pltpu.SMEM)
    _, ctx, dim = k_blk.shape
    return pl.pallas_call(
        functools.partial(attend_kernel, first, count),
        out_shape=(
            jax.ShapeDtypeStruct(k_blk.shape, BF16),
            jax.ShapeDtypeStruct(v_blk.shape, BF16),
            jax.ShapeDtypeStruct((2, count, 2048), BF16),
        ),
        in_specs=[smem, vm, vm, hbm, hbm] + [hbm] * len(prior),
        out_specs=(hbm, hbm, vm),
        input_output_aliases={5: 0, 6: 1} if prior else {},
        scratch_shapes=[
            VMEM((SLOTS, ctx, dim), BF16), VMEM((SLOTS, ctx, dim), BF16),
            VMEM((32, ctx), F32), VMEM((count, 32, dim), F32),
            DMA((SLOTS, 2)), DMA((SLOTS, 2)),
        ],
        cost_estimate=pl.CostEstimate(flops=count * 32 * ctx * dim * 4, bytes_accessed=count * ctx * dim * 8, transcendentals=count * 32 * ctx),
        compiler_params=pltpu.CompilerParams(vmem_limit_bytes=60 * 2 ** 20),
        name="attend",
    )(lens, q, kv, k_blk, v_blk, *prior)


def output_kernel(att_ref, act_own, act_far, x_ref, wo_h, wd_h, y_out,
                  wo_v, wd_v, attf, act_r, acc, ysend, yrecv,
                  wo_sem, wd_sem, a_ssem, a_rsem, f_ssem, f_rsem, c_ssem, c_rsem, y_ssem, y_rsem):
    row, col, chip, core = here()
    partner = col + 1 - 2 * core
    far = (col + 2) % 4
    far_partner = (partner + 2) % 4
    order = (col, far, partner, far_partner)
    wd_cp = []
    for s, owner in enumerate(order):
        wd_cp.append(pltpu.make_async_copy(wd_h.at[pl.ds(pl.multiple_of(owner * 2048, 2048), 2048), :], wd_v.at[s], wd_sem.at[s]))
    wo_cp = pltpu.make_async_copy(wo_h, wo_v, wo_sem)
    for cp in wd_cp + [wo_cp]:
        cp.start()

    greet_all()
    mine = row * 2 + chip
    a_cp = []
    for s, (dy, dx) in enumerate(((0, 1), (1, 0), (1, 1))):
        ty, xx = (row + dy) % 2, (chip + dx) % 2
        cp = remote(att_ref.at[ty], attf.at[mine, core], a_ssem.at[s], a_rsem.at[s], ty, xx * 2 + core)
        cp.start()
        a_cp.append(cp)
    c_cp = [remote(src, act_r.at[s], c_ssem.at[s], c_rsem.at[s], row, partner) for s, src in enumerate((act_own, act_far))]
    for cp in c_cp:
        cp.start()
    attf[mine, core] = att_ref[row]
    f_own = remote(attf.at[mine, core], attf.at[mine, core], f_ssem.at[3], f_rsem.at[3], row, partner)
    f_own.start()

    def mlp_part(s, act, cols):
        out = None
        for n in range(8):
            part = dot(act[n], wd_v[s, 256 * n:256 * n + 256, cols])
            out = part if out is None else out + part
        return out

    for s, act in ((0, act_own), (1, act_far)):
        wd_cp[s].wait()
        for c in range(4):
            cols = slice(256 * c, 256 * c + 256)
            part = mlp_part(s, act, cols)
            acc[:, cols] = part if s == 0 else acc[:, cols] + part

    f_cp = []
    for s, (dy, dx) in enumerate(((0, 1), (1, 0), (1, 1))):
        a_cp[s].wait_recv()
        index = ((row + dy) % 2) * 2 + (chip + dx) % 2
        cp = remote(attf.at[index, core], attf.at[index, core], f_ssem.at[s], f_rsem.at[s], row, partner)
        cp.start()
        f_cp.append(cp)
    for cp in c_cp:
        cp.wait_recv()
    wd_cp[2].wait()
    wd_cp[3].wait()
    for c in range(4):
        cols = slice(256 * c, 256 * c + 256)
        acc[:, cols] = acc[:, cols] + (mlp_part(2, act_r.at[0], cols) + mlp_part(3, act_r.at[1], cols))
    wo_cp.wait()
    for cp in f_cp + [f_own]:
        cp.wait_recv()
    y_cp = []
    for c in range(4):
        cols = slice(256 * c, 256 * c + 256)
        att = attf[...].reshape(128, 2048)
        ysend[c] = (acc[:, cols] + dot(att, wo_v[:, cols])).astype(BF16)
        cp = remote(ysend.at[c], yrecv.at[c], y_ssem.at[c], y_rsem.at[c], 1 - row, col)
        cp.start()
        y_cp.append(cp)
    for c in range(4):
        cols = slice(256 * c, 256 * c + 256)
        y_cp[c].wait_recv()
        both = ysend[c].astype(F32) + yrecv[c].astype(F32)
        y_out[:, cols] = (x_ref[:, cols].astype(F32) + both).astype(BF16)
    for cp in a_cp + c_cp + f_cp + [f_own] + y_cp:
        cp.wait_send()


def output(att, act_own, act_far, x_blk, w_out, w_down):
    rows, width = x_blk.shape
    vm = pl.BlockSpec(memory_space=VMEM)
    hbm = pl.BlockSpec(memory_space=pl.ANY)
    return pl.pallas_call(
        output_kernel,
        out_shape=jax.ShapeDtypeStruct((rows, width), BF16),
        in_specs=[vm] * 4 + [hbm] * 2,
        out_specs=vm,
        scratch_shapes=[
            VMEM((2048, width), BF16), VMEM((4, 2048, width), BF16), VMEM((4, 2, 16, 2048), BF16), VMEM((2, 8, rows, 256), BF16),
            VMEM((rows, width), F32), VMEM((4, rows, 256), BF16), VMEM((4, rows, 256), BF16),
            DMA, DMA((4,)), DMA((3,)), DMA((3,)), DMA((4,)), DMA((4,)), DMA((2,)), DMA((2,)), DMA((4,)), DMA((4,)),
        ],
        compiler_params=pltpu.CompilerParams(collective_id=1, has_side_effects=True, vmem_limit_bytes=40 * 2 ** 20),
        name="output",
    )(att, act_own, act_far, x_blk, w_out, w_down)


def solution(mesh):
    cache_spec = P(("dp", "ty", "tx"), None, None)
    across = [(0, 2), (1, 3), (2, 0), (3, 1)]

    def layer_shard(x_blk, lens, k_blk, v_blk, gamma, w_query, w_key, w_value, w_gate, w_up, w_out, w_down):
        half = 64
        inv_freqs = ROPE_BASE ** (-(jnp.arange(half, dtype=F32) * 2.0) / (2 * half))
        angles = lens.astype(F32)[:, None] * inv_freqs[None, :]
        cos, sin = jnp.cos(angles), jnp.sin(angles)
        cos2 = jnp.concatenate([cos, cos], axis=1)
        sin2 = jnp.concatenate([-sin, sin], axis=1)
        q, kv, keep, xs = project(x_blk, gamma[None, :], cos2, sin2, w_query, w_key, w_value, w_gate, w_up)
        got = lax.ppermute(xs, "tx", across)
        k_half, v_half, att_a = attend(0, FIRST, lens, q, kv, k_blk, v_blk)
        got, att_a = lax.optimization_barrier((got, att_a))
        full = (keep.astype(F32) + got.astype(F32)).astype(BF16).astype(F32)
        act = (jax.nn.silu(full[0]) * full[1]).astype(BF16)
        act_far = lax.ppermute(act, "tx", across)
        lens, act = lax.optimization_barrier((lens, act))
        k_out, v_out, att_b = attend(FIRST, 16 - FIRST, lens, q, kv, k_blk, v_blk, (k_half, v_half))
        att = jnp.concatenate([att_a, att_b], axis=1)
        y = output(att, act, act_far, x_blk, w_out, w_down)
        return y, k_out, v_out

    in_specs = (P("dp", "tx"), P("dp"), cache_spec, cache_spec, P("tx"), P("tx", "ty"), P("tx", None), P("tx", None), P("tx", "ty"), P("tx", "ty"), P("ty", "tx"), P("ty", "tx"))
    out_specs = (P("dp", "tx"), cache_spec, cache_spec)
    return jax.shard_map(layer_shard, mesh=mesh, in_specs=in_specs, out_specs=out_specs, check_vma=False)
```

time: 246 us -> 81.3 us (0.33)
  waiting for transfers between devices: 118 us -> 7.21 us
  Pallas kernels: 0 us -> 64.2 us
  matrix products: 50.1 us -> 0 us
  other arithmetic: 36.1 us -> 3.22 us
  blocking collectives: 17.8 us -> 0 us
  between operations: 13.9 us -> 0.7 us
  starting transfers between devices: 7.06 us -> 2.92 us
    psum x3 -> x0, waiting for transfers between devices: 118 us -> none  [the longest x2 98.4 us: layer_shard(): q_sum, k_sum, v_new, gate, up_proj = lax.psum(partials, 'tx')]
    pallas_call x0 -> x4, Pallas kernels: none -> 64.2 us  [the longest x2 27.4 us: attend(): pl.pallas_call(functools.partial(attend_kernel, first, count), out_shape=...]
    dot_general x9 -> x0, matrix products: 50.1 us -> none  [the longest x5 18.2 us: layer_shard(): jnp.dot(normed, weight, preferred_element_type=jnp.float32)]
    select_n x1 -> x0, other arithmetic: 23.3 us -> none  [layer_shard(): v_out = jnp.where(at_slot, v_own[:, None, :], v_blk)]
    all_gather x1 -> x0, blocking collectives: 9.04 us -> none  [layer_shard(): lax.all_gather(att_column, 'tx', axis=1, tiled=False)]
    psum x1 -> x0, blocking collectives: 8.75 us -> none  [layer_shard(): row_stats = lax.psum(row_stats, 'tx')]
    ppermute x0 -> x2, waiting for transfers between devices: none -> 7.21 us  [the longest x1 7 us: layer_shard(): got = lax.ppermute(xs, 'tx', across)]
    all_to_all x2 -> x0, starting transfers between devices: 6.94 us -> none  [the longest x1 3.56 us: layer_shard(): q_owned = lax.all_to_all(q_column, 'ty', 0, 0, tiled=True)]
  transfers between devices with their start and end apart: 5 -> 2, of which waited for: 3 -> 2; matrix products, arithmetic and copies ran while one was open for 20% -> 1% of each run, Pallas kernels for 0% -> 34%
where the time goes in v1:
time: 81.3 us; the launch traced here: 81.1 us
  Pallas kernels  64.2 us (79%)
  waiting for transfers between devices  7.21 us (9%)
  other arithmetic  3.22 us (4%)
  starting transfers between devices  2.92 us (4%)
  local copies, waits for them, and re-layouts  2.9 us (4%)
    pallas_call x2, Pallas kernels, attend(): pl.pallas_call(functools.partial(attend_kernel, first, count), out_shape=...  27.4 us
    pallas_call x1, Pallas kernels, project(): pl.pallas_call(project_kernel, out_shape=(jax.ShapeDtypeStruct((2, 16, 16...  20.5 us
    pallas_call x1, Pallas kernels, output(): pl.pallas_call(output_kernel, out_shape=jax.ShapeDtypeStruct((rows, width...  16.3 us
    ppermute x1, waiting for transfers between devices, layer_shard(): got = lax.ppermute(xs, 'tx', across)  7 us
    unnamed x9, local copies, waits for them, and re-layouts  2.9 us
  transfers between devices with their start and end apart: 2, of which 2 were waited for; matrix products, arithmetic and copies ran while one was open for 1% of the time, Pallas kernels for 34%

profile of v1, /device:TPU:0, one launch (start us, length us, event | category | flops | bytes accessed | tf_op | source)
XLA Modules:
  0.0 81.1 jit_solution(16424749190113599450)
XLA Ops:
  0.6 0.7 convert_element_type.18
  1.3 0.3 fusion.3
  1.6 0.8 pad_maximum_fusion.1
  2.4 20.5 %project.1 = (bf16[2,16,16,128]{3,2,1,0:T(8,128)(2,1)}, f32[2,16,128]{2,1,0:T(8,128)}, bf16[2,8,128,256]{3,2,1,0:T(8,128)(2,1)}, bf16[2,8,128,256]{3,2,1,0:T(8,128)(2,1)}) custom-call(bf16[128,1024]{1,0:T(8,128)(2,1)} %x_ref.3, f32[1,1024]{1,0:T(1,128)} %bitcast.11, f32[128,128]{1,0:T(8,128)} %get-tuple-element.34.cos_ref, ...), custom_call_target="tpu_custom_call" | custom-call | tf_op jit(solution)/shard_map/project/pallas_call | solution.py:195
  22.9 1.5 %collective-permute-start = (bf16[2,8,128,256]{3,2,1,0:T(8,128)(2,1)}, bf16[2,8,128,256]{3,2,1,0:T(8,128)(2,1)S(1)}, u32[]{:S(2)}, u32[]{:S(2)}) collective-permute-start(bf16[2,8,128,256]{3,2,1,0:T(8,128)(2,1)} %get-tuple-element.17), channel_id=1, source_target_pairs={{0,2},{1,3},{2,0},{3,1},{4,6},{5,7},{6,4},{7,5}} | collective-permute-start | bytes 3145736 | tf_op jit(solution)/shard_map/ppermute | solution.py:456
  24.3 0.0 copy-start.2
  24.3 16.8 %attend.2 = (bf16[16,4096,128]{2,1,0:T(8,128)(2,1)}, bf16[16,4096,128]{2,1,0:T(8,128)(2,1)}, bf16[2,10,2048]{2,1,0:T(8,128)(2,1)}) custom-call(s32[128]{0:T(128)} %lens_ref.2, bf16[2,16,16,128]{3,2,1,0:T(8,128)(2,1)} %get-tuple-element.18.q_ref, f32[2,16,128]{2,1,0:T(8,128)} %get-tuple-element.19.kv_ref, bf16[16,4096,128]{2,1,0:T(8,128)(2,1)} %k_in.3, ...), custom_call_target="tpu_custom_call" | custom-call | flops 671088640 | bytes 41943040 | tf_op jit(solution)/shard_map/attend/pallas_call | solution.py:326
  41.1 7.0 %collective-permute-done = bf16[2,8,128,256]{3,2,1,0:T(8,128)(2,1)S(1)} collective-permute-done((bf16[2,8,128,256]{3,2,1,0:T(8,128)(2,1)}, bf16[2,8,128,256]{3,2,1,0:T(8,128)(2,1)S(1)}, u32[]{:S(2)}, u32[]{:S(2)}) %collective-permute-start) | collective-permute-done | bytes 1048608 | tf_op jit(solution)/shard_map/ppermute | solution.py:456
  48.1 0.0 copy-done.2
  48.1 0.3 fusion
  48.4 0.3 fusion.2.act_own
  48.7 1.5 %collective-permute-start.1 = (bf16[8,128,256]{2,1,0:T(8,128)(2,1)S(1)}, bf16[8,128,256]{2,1,0:T(8,128)(2,1)S(1)}, u32[]{:S(2)}, u32[]{:S(2)}) collective-permute-start(bf16[8,128,256]{2,1,0:T(8,128)(2,1)S(1)} %fusion.2.act_own), channel_id=1, source_target_pairs={{0,2},{1,3},{2,0},{3,1},{4,6},{5,7},{6,4},{7,5}} | collective-permute-start | bytes 1572872 | tf_op jit(solution)/shard_map/ppermute | solution.py:461
  50.2 0.0 copy-start.3
  50.2 0.0 copy-start.1
  50.2 10.6 %attend.3 = (bf16[16,4096,128]{2,1,0:T(8,128)(2,1)}, bf16[16,4096,128]{2,1,0:T(8,128)(2,1)}, bf16[2,6,2048]{2,1,0:T(8,128)(2,1)}) custom-call(s32[128]{0:T(128)} %lens_ref.2, bf16[2,16,16,128]{3,2,1,0:T(8,128)(2,1)} %get-tuple-element.18.q_ref, f32[2,16,128]{2,1,0:T(8,128)} %get-tuple-element.19.kv_ref, ...), custom_call_target="tpu_custom_call", output_to_operand_aliasing={{0}: (5, {}), {1}: (6, {})} | custom-call | flops 402653184 | bytes 25165824 | tf_op jit(solution)/shard_map/attend/pallas_call | solution.py:326
  60.8 0.0 copy-done.3
  60.8 0.9 %pad_maximum_fusion.att_ref = bf16[2,16,2048]{2,1,0:T(8,128)(2,1)S(1)} fusion(bf16[2,6,2048]{2,1,0:T(8,128)(2,1)} %get-tuple-element.27, bf16[2,10,2048]{2,1,0:T(8,128)(2,1)S(1)} %copy-done.3), kind=kLoop, calls=%fused_computation.6 | loop fusion | flops 262144 | bytes 262144 | tf_op jit(solution)/shard_map/concatenate | solution.py:464
  61.7 0.2 collective-permute-done.1.act_far
  61.9 0.0 copy-done.1
  61.9 0.0 copy-start
  61.9 2.2 %copy-done = bf16[2048,1024]{1,0:T(8,128)(2,1)S(1)} copy-done((bf16[2048,1024]{1,0:T(8,128)(2,1)S(1)}, bf16[2048,1024]{1,0:T(8,128)(2,1)}, u32[]{:S(2)}) %copy-start) | copy-done | bytes 4194328
  64.1 16.3 %output.1 = bf16[128,1024]{1,0:T(8,128)(2,1)S(1)} custom-call(bf16[2,16,2048]{2,1,0:T(8,128)(2,1)S(1)} %pad_maximum_fusion.att_ref, bf16[8,128,256]{2,1,0:T(8,128)(2,1)S(1)} %fusion.2.act_own, bf16[8,128,256]{2,1,0:T(8,128)(2,1)S(1)} %collective-permute-done.1.act_far, bf16[128,1024]{1,0:T(8,128)(2,1)S(1)} %copy-done.1, bf16[2048,1024]{1,0:T(8,128)(2,1)S(1)} %copy-done, ...), custom_call_target="tpu_custom_call" | custom-call | tf_op jit(solution)/shard_map/output/pallas_call | solution.py:429
  80.4 0.7 copy.20
  (1 shorter events, 0.0 us)
Async XLA Ops:
  22.9 25.3 %collective-permute-start = (bf16[2,8,128,256]{3,2,1,0:T(8,128)(2,1)}, bf16[2,8,128,256]{3,2,1,0:T(8,128)(2,1)S(1)}, u32[]{:S(2)}, u32[]{:S(2)}) collective-permute-start(bf16[2,8,128,256]{3,2,1,0:T(8,128)(2,1)} %get-tuple-element.17), channel_id=1, source_target_pairs={{0,2},{1,3},{2,0},{3,1},{4,6},{5,7},{6,4},{7,5}} | collective-permute-start | bytes 3145736 | tf_op jit(solution)/shard_map/ppermute | solution.py:456
  24.3 23.8 %copy-start.2 = (bf16[2,8,128,256]{3,2,1,0:T(8,128)(2,1)S(1)}, bf16[2,8,128,256]{3,2,1,0:T(8,128)(2,1)}, u32[]{:S(2)}) copy-start(bf16[2,8,128,256]{3,2,1,0:T(8,128)(2,1)} %get-tuple-element.22) | copy-start | bytes 3145732
  48.7 13.2 %collective-permute-start.1 = (bf16[8,128,256]{2,1,0:T(8,128)(2,1)S(1)}, bf16[8,128,256]{2,1,0:T(8,128)(2,1)S(1)}, u32[]{:S(2)}, u32[]{:S(2)}) collective-permute-start(bf16[8,128,256]{2,1,0:T(8,128)(2,1)S(1)} %fusion.2.act_own), channel_id=1, source_target_pairs={{0,2},{1,3},{2,0},{3,1},{4,6},{5,7},{6,4},{7,5}} | collective-permute-start | bytes 1572872 | tf_op jit(solution)/shard_map/ppermute | solution.py:461
  50.2 10.6 %copy-start.3 = (bf16[2,10,2048]{2,1,0:T(8,128)(2,1)S(1)}, bf16[2,10,2048]{2,1,0:T(8,128)(2,1)}, u32[]{:S(2)}) copy-start(bf16[2,10,2048]{2,1,0:T(8,128)(2,1)} %get-tuple-element.21) | copy-start | bytes 245764
  50.2 11.7 %copy-start.1 = (bf16[128,1024]{1,0:T(8,128)(2,1)S(1)}, bf16[128,1024]{1,0:T(8,128)(2,1)}, u32[]{:S(2)}) copy-start(bf16[128,1024]{1,0:T(8,128)(2,1)} %x_ref.3) | copy-start | bytes 786436
  61.9 2.2 %copy-start = (bf16[2048,1024]{1,0:T(8,128)(2,1)S(1)}, bf16[2048,1024]{1,0:T(8,128)(2,1)}, u32[]{:S(2)}) copy-start(bf16[2048,1024]{1,0:T(8,128)(2,1)} %wo_h.1) | copy-start | bytes 12582916

commit v2 on v1

v2 whole, which is shorter than its diff:
```python
import functools

import jax
import jax.numpy as jnp
import numpy as np
from jax import lax
from jax.experimental import pallas as pl
from jax.experimental.pallas import tpu as pltpu
from jax.sharding import PartitionSpec as P

EPSILON = 1e-6
ROPE_BASE = 10000.0
BF16 = jnp.bfloat16
F32 = jnp.float32
MESH = pl.DeviceIdType.MESH

VMEM = pltpu.VMEM
VMEM_ALL = 67043328
DMA = pltpu.SemaphoreType.DMA


def here():
    row = lax.axis_index("ty")
    col = lax.axis_index("tx")
    return row, col, col // 2, col % 2


def greet():
    row, col, _, _ = here()
    me = row * 4 + col
    barrier = pltpu.get_barrier_semaphore()
    for step in range(1, 8):
        peer = (me + step) % 8
        pl.semaphore_signal(barrier, inc=1, device_id={"ty": peer // 4, "tx": peer % 4}, device_id_type=MESH)


def greeted():
    pl.semaphore_wait(pltpu.get_barrier_semaphore(), 7)


def remote(src, dst, send_sem, recv_sem, ty, tx):
    return pltpu.make_async_remote_copy(
        src_ref=src, dst_ref=dst, send_sem=send_sem, recv_sem=recv_sem,
        device_id={"ty": ty, "tx": tx}, device_id_type=MESH)


def dot(a, b):
    return jnp.dot(a, b, preferred_element_type=F32)


CHUNKS = 8


def gated(g, u):
    return (jax.nn.silu(g.astype(BF16).astype(F32)) * u.astype(BF16).astype(F32)).astype(BF16)


def project_kernel(lens_h, x_h, gamma_h, freq_h, wq_h, wk_h, wv_h, wg_h, wu_h,
                   q_hbm, kv_hbm, keep_hbm, pay_hbm,
                   lens_ref, freq_ref, q_out, kv_out, keep_out, pay_out, res_sem, keep_sem, x_ref, gamma_ref, x_sem, wq_v, wkv_v, wg_v, wu_v, h_v, st_send, st_recv,
                   qp, qd, qx, qr, kvp, kvr, qscr, dsend, drecv, own,
                   wq_sem, wkv_sem, w_sem, st_ssem, st_rsem, qd_ssem, qd_rsem, q_ssem, q_rsem,
                   kv_ssem, kv_rsem, d_ssem, d_rsem):
    row, col, chip, core = here()
    partner = col + 1 - 2 * core
    me = row * 4 + col
    greet()

    x_cp = pltpu.make_async_copy(x_h, x_ref, x_sem.at[0])
    gamma_cp = pltpu.make_async_copy(gamma_h, gamma_ref, x_sem.at[1])
    lens_cp = pltpu.make_async_copy(lens_h, lens_ref, x_sem.at[2])
    freq_cp = pltpu.make_async_copy(freq_h, freq_ref, x_sem.at[3])
    for cp in (x_cp, gamma_cp, lens_cp, freq_cp):
        cp.start()
    wq_cp = [pltpu.make_async_copy(wq_h.at[:, pl.ds(512 * p, 512)], wq_v.at[p], wq_sem.at[p]) for p in range(4)]
    kv_cp = [pltpu.make_async_copy(w.at[:, :], wkv_v.at[:, pl.ds(128 * p, 128)], wkv_sem.at[p]) for p, w in enumerate((wk_h, wv_h))]
    for cp in wq_cp + kv_cp:
        cp.start()

    def weight_copies(n):
        out = []
        for quarter in range(4):
            cols = pl.ds(pl.multiple_of(2048 * quarter + 256 * n, 256), 256)
            out.append(pltpu.make_async_copy(wg_h.at[:, cols], wg_v.at[n, quarter], w_sem.at[n, quarter, 0]))
            out.append(pltpu.make_async_copy(wu_h.at[:, cols], wu_v.at[n, quarter], w_sem.at[n, quarter, 1]))
        return out

    def start_weights(n, carry):
        for cp in weight_copies(n):
            cp.start()
        return carry

    lax.fori_loop(0, CHUNKS, start_weights, 0)

    x_cp.wait()
    xf = x_ref[...].astype(F32)
    sum1 = jnp.sum(xf, axis=1, keepdims=True)
    sum2 = jnp.sum(xf * xf, axis=1, keepdims=True)
    rows = xf.shape[0]
    eye = lax.broadcasted_iota(jnp.int32, (rows, rows), 0) == lax.broadcasted_iota(jnp.int32, (rows, rows), 1)
    line1 = jnp.sum(jnp.where(eye, sum1, 0.0), axis=0, keepdims=True)
    line2 = jnp.sum(jnp.where(eye, sum2, 0.0), axis=0, keepdims=True)
    first = lax.broadcasted_iota(jnp.int32, (8, rows), 0) == 0
    st_send[...] = jnp.where(first, line1, line2)
    greeted()
    st_cp = [remote(st_send, st_recv.at[d - 1], st_ssem.at[d - 1], st_rsem.at[d - 1], row, (col + d) % 4) for d in (1, 2, 3)]
    for cp in st_cp:
        cp.start()
    lens_cp.wait()
    freq_cp.wait()
    seq = lax.broadcasted_iota(jnp.int32, (16, 128), 0)
    place = jnp.zeros((16, 128), F32)
    for b in range(16):
        place = jnp.where(seq == b, lens_ref[me * 16 + b].astype(F32), place)
    angle = place * freq_ref[...]
    cosv = jnp.cos(angle)
    sinv = jnp.where(lax.broadcasted_iota(jnp.int32, (16, 128), 1) < 64, -jnp.sin(angle), jnp.sin(angle))
    for cp in st_cp:
        cp.wait_recv()
    total = st_send[...] + st_recv[0] + st_recv[1] + st_recv[2]
    width = 4.0 * xf.shape[1]
    mean_line = total[0:1] / width
    var_line = total[1:2] / width - mean_line * mean_line
    rstd_line = lax.rsqrt(var_line + EPSILON)
    mean = jnp.sum(jnp.where(eye, mean_line, 0.0), axis=1, keepdims=True)
    rstd = jnp.sum(jnp.where(eye, rstd_line, 0.0), axis=1, keepdims=True)
    gamma_cp.wait()
    h_v[...] = ((xf - mean) * rstd * gamma_ref[...]).astype(BF16)

    for cp in wq_cp:
        cp.wait()
    for p in range(4):
        part = dot(h_v[...], wq_v[p]).astype(BF16)
        for d in range(8):
            qp[d % 2, d // 2, :, 512 * p:512 * p + 512] = part[16 * d:16 * d + 16]
    qd_cp = remote(qp.at[1 - core], qd, qd_ssem, qd_rsem, row, partner)
    qd_cp.start()
    for cp in kv_cp:
        cp.wait()
    kvp[...] = dot(h_v[...], wkv_v[...]).reshape(8, 16, 256)
    kv_sends = []
    for d in (1, 2, 3):
        peer = (col + d) % 4
        cp = remote(kvp.at[row * 4 + peer], kvr.at[d - 1], kv_ssem.at[d - 1], kv_rsem.at[d - 1], row, peer)
        cp.start()
        kv_sends.append(cp)

    def pair_copy(n):
        return remote(dsend.at[n], drecv.at[n], d_ssem.at[n], d_rsem.at[n], row, partner)

    def compute_chunk(n):
        for cp in weight_copies(n):
            cp.wait()
        for xr in range(2):
            quarter = 2 * xr + (1 - core)
            dsend[n, xr, 0] = dot(h_v[...], wg_v[n, quarter]).astype(BF16)
            dsend[n, xr, 1] = dot(h_v[...], wu_v[n, quarter]).astype(BF16)
        pair_copy(n).start()
        for xr in range(2):
            quarter = 2 * xr + core
            own[n % 3, xr, 0] = dot(h_v[...], wg_v[n, quarter])
            own[n % 3, xr, 1] = dot(h_v[...], wu_v[n, quarter])

    def sum_chunk(n):
        pair_copy(n).wait_recv()
        keep = own[n % 3, chip] + drecv[n, chip].astype(F32)
        give = (own[n % 3, 1 - chip] + drecv[n, 1 - chip].astype(F32)).astype(BF16)
        return keep, give

    def sum_late(n):
        keep, give = sum_chunk(n)
        for part in range(2):
            keep_out[part * CHUNKS + n] = keep[part].astype(BF16)
            pay_out[part * CHUNKS + n] = give[part]
        for cp in late_copies(n):
            cp.start()

    def late_copies(m):
        out = []
        for part in range(2):
            block = part * CHUNKS + m
            out.append(pltpu.make_async_copy(keep_out.at[block], keep_hbm.at[block], keep_sem.at[block, 0]))
            out.append(pltpu.make_async_copy(pay_out.at[block], pay_hbm.at[block], keep_sem.at[block, 1]))
        return out

    compute_chunk(0)

    qd_cp.wait_recv()
    qx[...] = (qp[core].astype(F32) + qd[...].astype(F32)).astype(BF16)
    mine = row * 2 + chip
    q_sends = []
    for s, (dy, dx) in enumerate(((0, 1), (1, 0), (1, 1))):
        ty, xx = (row + dy) % 2, (chip + dx) % 2
        cp = remote(qx.at[ty * 2 + xx], qr.at[s], q_ssem.at[s], q_rsem.at[s], ty, xx * 2 + core)
        cp.start()
        q_sends.append(cp)

    compute_chunk(1)

    def step(n, carry):
        compute_chunk(n)
        sum_late(n - 2)
        return carry

    lax.fori_loop(2, CHUNKS, step, 0)
    sum_late(CHUNKS - 2)

    def rotate(vals):
        return vals * cosv + pltpu.roll(vals, 64, 1) * sinv

    for cp in q_sends:
        cp.wait_recv()
    q_same = qx[mine].astype(F32) + qr[0].astype(F32)
    q_diff = qr[1].astype(F32) + qr[2].astype(F32)
    for half, vals in ((row, q_same), (1 - row, q_diff)):
        for head in range(16):
            qscr[half, :, head, :] = rotate(vals[:, 128 * head:128 * head + 128])
    q_out[...] = qscr[...].astype(BF16)
    q_cp = pltpu.make_async_copy(q_out, q_hbm, res_sem.at[0])
    q_cp.start()
    for cp in kv_sends:
        cp.wait_recv()
    kv = kvp[me] + kvr[0] + kvr[1] + kvr[2]
    kv_out[0] = rotate(kv[:, :128]).astype(BF16).astype(F32)
    kv_out[1] = kv[:, 128:].astype(BF16).astype(F32)

    kv_cp = pltpu.make_async_copy(kv_out, kv_hbm, res_sem.at[1])
    kv_cp.start()
    sum_late(CHUNKS - 1)
    for cp in (q_cp, kv_cp):
        cp.wait()
    for m in range(CHUNKS):
        for cp in late_copies(m):
            cp.wait()
    for cp in st_cp + [qd_cp] + kv_sends + q_sends:
        cp.wait_send()

    def drain(n, carry):
        pair_copy(n).wait_send()
        return carry

    lax.fori_loop(0, CHUNKS, drain, 0)


def project(lens, x_blk, gamma, freqs, w_query, w_key, w_value, w_gate, w_up):
    rows, width = x_blk.shape
    nc = CHUNKS
    hbm = pl.BlockSpec(memory_space=pl.ANY)
    return pl.pallas_call(
        project_kernel,
        out_shape=(
            jax.ShapeDtypeStruct((2, 16, 16, 128), BF16),
            jax.ShapeDtypeStruct((2, 16, 128), F32),
            jax.ShapeDtypeStruct((2 * CHUNKS, rows, 256), BF16),
            jax.ShapeDtypeStruct((2 * CHUNKS, rows, 256), BF16),
        ),
        in_specs=[hbm] * 9,
        out_specs=(hbm,) * 4,
        scratch_shapes=[
            pltpu.SMEM((128,), jnp.int32), VMEM((1, 128), F32), VMEM((2, 16, 16, 128), BF16), VMEM((2, 16, 128), F32),
            VMEM((2 * CHUNKS, rows, 256), BF16), VMEM((2 * CHUNKS, rows, 256), BF16),
            DMA((2,)), DMA((2 * CHUNKS, 2)),
            VMEM((rows, width), BF16), VMEM((1, width), F32), DMA((4,)),
            VMEM((4, width, 512), BF16), VMEM((width, 256), BF16),
            VMEM((nc, 4, width, 256), BF16), VMEM((nc, 4, width, 256), BF16),
            VMEM((rows, width), BF16), VMEM((8, rows), F32), VMEM((3, 8, rows), F32),
            VMEM((2, 4, 16, 2048), BF16), VMEM((4, 16, 2048), BF16), VMEM((4, 16, 2048), BF16), VMEM((3, 16, 2048), BF16),
            VMEM((8, 16, 256), F32), VMEM((3, 16, 256), F32), VMEM((2, 16, 16, 128), F32),
            VMEM((nc, 2, 2, rows, 256), BF16), VMEM((nc, 2, 2, rows, 256), BF16), VMEM((3, 2, 2, rows, 256), F32),
            DMA((4,)), DMA((2,)), DMA((nc, 4, 2)), DMA((3,)), DMA((3,)), DMA, DMA, DMA((3,)), DMA((3,)),
            DMA((3,)), DMA((3,)), DMA((nc,)), DMA((nc,)),
        ],
        compiler_params=pltpu.CompilerParams(collective_id=0, has_side_effects=True, vmem_limit_bytes=VMEM_ALL),
        name="project",
    )(lens, x_blk, gamma, freqs, w_query, w_key, w_value, w_gate, w_up)


SLOTS = 12
AHEAD = 7
BLOCK = 1024


def attend_kernel(lens_h, q_h, kv_h, k_in, v_in, k_out, v_out, att_hbm,
                  kbuf, vbuf, s_scr, in_sem, out_sem, att_out, lens_ref, q_ref, kv_ref, o_scr, small_sem):
    row, col, _, _ = here()
    base = (row * 4 + col) * 16
    count, ctx, _ = k_in.shape

    def in_copies(t):
        slot = lax.rem(t, SLOTS)
        return (pltpu.make_async_copy(k_in.at[t], kbuf.at[slot], in_sem.at[slot, 0]),
                pltpu.make_async_copy(v_in.at[t], vbuf.at[slot], in_sem.at[slot, 1]))

    def out_copies(t):
        slot = lax.rem(t, SLOTS)
        return (pltpu.make_async_copy(kbuf.at[slot], k_out.at[t], out_sem.at[slot, 0]),
                pltpu.make_async_copy(vbuf.at[slot], v_out.at[t], out_sem.at[slot, 1]))

    small = [pltpu.make_async_copy(src, dst, small_sem.at[s]) for s, (src, dst) in enumerate(((lens_h, lens_ref), (q_h, q_ref), (kv_h, kv_ref)))]
    for cp in small:
        cp.start()
    for t in range(min(AHEAD, count)):
        for cp in in_copies(t):
            cp.start()
    for cp in small:
        cp.wait()

    def attend(t, slot, length, blocks):
        q = jnp.concatenate([q_ref[0, t], q_ref[1, t]], axis=0)
        scale = 128.0 ** -0.5
        peak = None
        for b in range(blocks):
            scores = lax.dot_general(q, kbuf[slot, b * BLOCK:(b + 1) * BLOCK, :], (((1,), (1,)), ((), ())),
                                     preferred_element_type=F32) * scale
            if b == blocks - 1:
                pos = lax.broadcasted_iota(jnp.int32, scores.shape, 1) + b * BLOCK
                scores = jnp.where(pos <= length, scores, -1e30)
            s_scr[:, b * BLOCK:(b + 1) * BLOCK] = scores
            for g in range(BLOCK // 128):
                piece = scores[:, g * 128:(g + 1) * 128]
                peak = piece if peak is None else jnp.maximum(peak, piece)
        peak = jnp.max(peak, axis=1, keepdims=True)
        denom = None
        for b in range(blocks):
            e = jnp.exp(s_scr[:, b * BLOCK:(b + 1) * BLOCK] - peak)
            s_scr[:, b * BLOCK:(b + 1) * BLOCK] = e
            for g in range(BLOCK // 128):
                piece = e[:, g * 128:(g + 1) * 128]
                denom = piece if denom is None else denom + piece
        inv = 1.0 / jnp.sum(denom, axis=1, keepdims=True)
        out = None
        for b in range(blocks):
            probs = (s_scr[:, b * BLOCK:(b + 1) * BLOCK] * inv).astype(BF16)
            part = dot(probs, vbuf[slot, b * BLOCK:(b + 1) * BLOCK, :])
            out = part if out is None else out + part
        o_scr[t] = out

    def body(t, carry):
        slot = lax.rem(t, SLOTS)
        for cp in in_copies(t):
            cp.wait()
        length = lens_ref[base + t]
        start = pl.multiple_of((length // 16) * 16, 16)
        at_row = lax.broadcasted_iota(jnp.int32, (16, 128), 0) == length - start
        for which, buf in ((0, kbuf), (1, vbuf)):
            old = buf[slot, pl.ds(start, 16), :].astype(F32)
            new = kv_ref[which, pl.ds(t, 1), :]
            buf[slot, pl.ds(start, 16), :] = jnp.where(at_row, new, old).astype(BF16)
        for cp in out_copies(t):
            cp.start()

        @pl.when(t + AHEAD < count)
        def _():
            @pl.when(t >= SLOTS - AHEAD)
            def _():
                for cp in out_copies(t - (SLOTS - AHEAD)):
                    cp.wait()

            for cp in in_copies(t + AHEAD):
                cp.start()

        blocks = length // BLOCK
        for b in range(ctx // BLOCK):
            @pl.when(blocks == b)
            def _():
                attend(t, slot, length, b + 1)

        return carry

    lax.fori_loop(0, count, body, 0)

    for head in range(32):
        att_out[head // 16, :, 128 * (head % 16):128 * (head % 16) + 128] = o_scr[:, head, :].astype(BF16)
    res = pltpu.make_async_copy(att_out, att_hbm, small_sem.at[3])
    res.start()
    done_in_loop = max(0, count - AHEAD - (SLOTS - AHEAD)) if count > AHEAD else 0
    for t in range(done_in_loop, count):
        for cp in out_copies(t):
            cp.wait()
    res.wait()


def attend(lens, q, kv, k_blk, v_blk):
    hbm = pl.BlockSpec(memory_space=pltpu.HBM)
    count, ctx, dim = k_blk.shape
    return pl.pallas_call(
        attend_kernel,
        out_shape=(
            jax.ShapeDtypeStruct(k_blk.shape, BF16),
            jax.ShapeDtypeStruct(v_blk.shape, BF16),
            jax.ShapeDtypeStruct((2, count, 2048), BF16),
        ),
        in_specs=[hbm] * 5,
        out_specs=(hbm,) * 3,
        scratch_shapes=[
            VMEM((SLOTS, ctx, dim), BF16), VMEM((SLOTS, ctx, dim), BF16),
            VMEM((32, ctx), F32), DMA((SLOTS, 2)), DMA((SLOTS, 2)), VMEM((2, count, 2048), BF16),
            pltpu.SMEM((128,), jnp.int32), VMEM((2, 16, 16, 128), BF16), VMEM((2, 16, 128), F32),
            VMEM((count, 32, dim), F32), DMA((4,)),
        ],
        cost_estimate=pl.CostEstimate(flops=count * 32 * ctx * dim * 4, bytes_accessed=count * ctx * dim * 8, transcendentals=count * 32 * ctx),
        compiler_params=pltpu.CompilerParams(vmem_limit_bytes=VMEM_ALL),
        name="attend",
    )(lens, q, kv, k_blk, v_blk)


HALF = 64
PIECES = 4


def output_kernel(att_h, keep_h, got_h, x_h, wo_h, wd_h, y_hbm,
                  att_ref, keep_v, got_v, x_ref, y_out, act_v, in_sem, wo_v, wd_v, attf, acc, ysend, yrecv,
                  wo_sem, wd_sem, a_ssem, a_rsem, f_ssem, f_rsem, g_ssem, g_rsem, h_ssem, h_rsem, c_ssem, c_rsem, y_ssem, y_rsem):
    greet()
    row, col, chip, core = here()
    partner = col + 1 - 2 * core
    far = (col + 2) % 4
    far_partner = (partner + 2) % 4
    order = (col, far, partner, far_partner)
    in_cp = [pltpu.make_async_copy(src, dst, in_sem.at[s]) for s, (src, dst) in enumerate(((att_h, att_ref), (keep_h, keep_v), (got_h, got_v), (x_h, x_ref)))]
    for cp in in_cp:
        cp.start()
    wd_cp = []
    for s, owner in enumerate(order):
        wd_cp.append(pltpu.make_async_copy(wd_h.at[pl.ds(pl.multiple_of(owner * 2048, 2048), 2048), :], wd_v.at[s], wd_sem.at[s]))
    wo_cp = pltpu.make_async_copy(wo_h, wo_v, wo_sem)

    in_cp[0].wait()
    greeted()
    mine = row * 2 + chip
    around = ((0, 1), (1, 0), (1, 1))
    a_cp = []
    for s, (dy, dx) in enumerate(around):
        ty, xx = (row + dy) % 2, (chip + dx) % 2
        cp = remote(att_ref.at[ty], attf.at[mine, core], a_ssem.at[s], a_rsem.at[s], ty, xx * 2 + core)
        cp.start()
        a_cp.append(cp)
    attf[mine, core] = att_ref[row]
    f_own = remote(attf.at[mine, core], attf.at[mine, core], f_ssem.at[3], f_rsem.at[3], row, partner)
    f_own.start()

    def piece(s, r, p):
        return act_v.at[s, r, :, pl.ds(512 * p, 512)]

    in_cp[1].wait()
    in_cp[2].wait()
    for cp in (wd_cp[0], wd_cp[2], wo_cp, wd_cp[1], wd_cp[3]):
        cp.start()
    g_cp, h_cp, c_cp = {}, {}, []
    for r in range(2):
        rows = slice(HALF * r, HALF * r + HALF)
        for p in range(PIECES):
            for n in (2 * p, 2 * p + 1):
                g = keep_v[n, rows].astype(F32) + got_v[n, rows].astype(F32)
                u = keep_v[CHUNKS + n, rows].astype(F32) + got_v[CHUNKS + n, rows].astype(F32)
                act_v[0, r, :, 256 * n:256 * n + 256] = gated(g, u)
            g_cp[r, p] = remote(piece(0, r, p), piece(1, r, p), g_ssem.at[r, p], g_rsem.at[r, p], row, far)
            g_cp[r, p].start()
            h_cp[r, p] = remote(piece(1, r, p), piece(3, r, p), h_ssem.at[r, p], h_rsem.at[r, p], row, partner)
        cp = remote(act_v.at[0, r], act_v.at[2, r], c_ssem.at[r], c_rsem.at[r], row, partner)
        cp.start()
        c_cp.append(cp)

    def whole(s):
        return act_v[s].reshape(2 * HALF, 2048)

    def add(lhs, rhs, first=False):
        for c in range(2):
            cols = slice(512 * c, 512 * c + 512)
            part = dot(lhs, rhs[:, cols])
            acc[:, cols] = part if first else acc[:, cols] + part

    wd_cp[0].wait()
    add(whole(0), wd_v.at[0], True)
    for cp in c_cp:
        cp.wait_recv()
    wd_cp[2].wait()
    add(whole(2), wd_v.at[2])
    f_cp = []
    for s, (dy, dx) in enumerate(around):
        a_cp[s].wait_recv()
        index = ((row + dy) % 2) * 2 + (chip + dx) % 2
        cp = remote(attf.at[index, core], attf.at[index, core], f_ssem.at[s], f_rsem.at[s], row, partner)
        cp.start()
        f_cp.append(cp)
    wo_cp.wait()
    for cp in f_cp + [f_own]:
        cp.wait_recv()
    add(attf[...].reshape(2 * HALF, 2048), wo_v)
    wd_cp[1].wait()
    wd_cp[3].wait()
    y_cp = {}
    for r in range(2):
        rows = slice(HALF * r, HALF * r + HALF)
        for p in range(PIECES):
            g_cp[r, p].wait_recv()
            h_cp[r, p].start()
        for p in range(PIECES):
            h_cp[r, p].wait_recv()
        for c in range(2):
            cols = slice(512 * c, 512 * c + 512)
            part = dot(act_v[1, r], wd_v[1, :, cols]) + dot(act_v[3, r], wd_v[3, :, cols])
            ysend[r, c] = (acc[rows, cols] + part).astype(BF16)
            y_cp[r, c] = remote(ysend.at[r, c], yrecv.at[r, c], y_ssem.at[r, c], y_rsem.at[r, c], 1 - row, col)
            y_cp[r, c].start()
    in_cp[3].wait()
    for r in range(2):
        rows = slice(HALF * r, HALF * r + HALF)
        for c in range(2):
            cols = slice(512 * c, 512 * c + 512)
            y_cp[r, c].wait_recv()
            both = ysend[r, c].astype(F32) + yrecv[r, c].astype(F32)
            y_out[rows, cols] = (x_ref[rows, cols].astype(F32) + both).astype(BF16)
    res = pltpu.make_async_copy(y_out, y_hbm, in_sem.at[0])
    res.start()
    for cp in a_cp + c_cp + f_cp + [f_own] + list(g_cp.values()) + list(h_cp.values()) + list(y_cp.values()):
        cp.wait_send()
    res.wait()


def output(att, keep, got, x_blk, w_out, w_down):
    rows, width = x_blk.shape
    hbm = pl.BlockSpec(memory_space=pl.ANY)
    return pl.pallas_call(
        output_kernel,
        out_shape=jax.ShapeDtypeStruct((rows, width), BF16),
        in_specs=[hbm] * 6,
        out_specs=hbm,
        scratch_shapes=[
            VMEM((2, 16, 2048), BF16), VMEM((2 * CHUNKS, rows, 256), BF16), VMEM((2 * CHUNKS, rows, 256), BF16),
            VMEM((rows, width), BF16), VMEM((rows, width), BF16),
            VMEM((4, 2, HALF, 256 * CHUNKS), BF16), DMA((4,)),
            VMEM((2048, width), BF16), VMEM((4, 2048, width), BF16), VMEM((4, 2, 16, 2048), BF16),
            VMEM((rows, width), F32), VMEM((2, 2, HALF, 512), BF16), VMEM((2, 2, HALF, 512), BF16),
            DMA, DMA((4,)), DMA((3,)), DMA((3,)), DMA((4,)), DMA((4,)), DMA((2, PIECES)), DMA((2, PIECES)), DMA((2, PIECES)), DMA((2, PIECES)),
            DMA((2,)), DMA((2,)), DMA((2, 2)), DMA((2, 2)),
        ],
        compiler_params=pltpu.CompilerParams(collective_id=1, has_side_effects=True, vmem_limit_bytes=VMEM_ALL),
        name="output",
    )(att, keep, got, x_blk, w_out, w_down)


def solution(mesh):
    cache_spec = P(("dp", "ty", "tx"), None, None)
    across = [(0, 2), (1, 3), (2, 0), (3, 1)]

    def layer_shard(x_blk, lens, k_blk, v_blk, gamma, w_query, w_key, w_value, w_gate, w_up, w_out, w_down):
        freqs = np.tile(np.float32(ROPE_BASE ** (-np.arange(0, 128, 2) / 128.0)), 2)[None, :]
        q, kv, keep, pay = project(lens, x_blk, gamma[None, :], freqs, w_query, w_key, w_value, w_gate, w_up)
        got = lax.ppermute(pay, "tx", across)
        k_out, v_out, att = attend(lens, q, kv, k_blk, v_blk)
        y = output(att, keep, got, x_blk, w_out, w_down)
        return y, k_out, v_out

    in_specs = (P("dp", "tx"), P("dp"), cache_spec, cache_spec, P("tx"), P("tx", "ty"), P("tx", None), P("tx", None), P("tx", "ty"), P("tx", "ty"), P("ty", "tx"), P("ty", "tx"))
    out_specs = (P("dp", "tx"), cache_spec, cache_spec)
    return jax.shard_map(layer_shard, mesh=mesh, in_specs=in_specs, out_specs=out_specs, check_vma=False)
```

time: 81.3 us -> 71.3 us (0.88)
  waiting for transfers between devices: 7.21 us -> 0.05 us
  other arithmetic: 3.22 us -> 0 us
  Pallas kernels: 64.2 us -> 67.4 us
  starting transfers between devices: 2.92 us -> 1.39 us
  local copies, waits for them, and re-layouts: 2.9 us -> 1.67 us
    pallas_call x1, Pallas kernels: 16.3 us -> 25 us  [output(): pl.pallas_call(output_kernel, out_shape=jax.ShapeDtypeStruct((rows, width...]
    ppermute x2 -> x1, waiting for transfers between devices: 7.21 us -> 0.05 us  [layer_shard(): got = lax.ppermute(pay, 'tx', across)]
    pallas_call x2 -> x1, Pallas kernels: 27.4 us -> 23.8 us  [attend(): pl.pallas_call(attend_kernel, out_shape=(jax.ShapeDtypeStruct(k_blk.shape...]
    pallas_call x1, Pallas kernels: 20.5 us -> 18.6 us  [project(): pl.pallas_call(project_kernel, out_shape=(jax.ShapeDtypeStruct((2, 16, 16...]
    concatenate x2 -> x0, other arithmetic: 1.64 us -> none  [the longest x1 0.88 us: layer_shard(): att = jnp.concatenate([att_a, att_b], axis=1)]
    ppermute x2 -> x1, starting transfers between devices: 2.92 us -> 1.39 us  [layer_shard(): got = lax.ppermute(pay, 'tx', across)]
    convert_element_type x3 -> x0, other arithmetic: 1.27 us -> none  [the longest x1 0.66 us: layer_shard(): angles = lens.astype(F32)[:, None] * inv_freqs[None, :]]
    unnamed x9 -> x1, local copies, waits for them, and re-layouts: 2.9 us -> 1.67 us
  transfers between devices with their start and end apart: 2 -> 1, of which waited for: 2 -> 0; matrix products, arithmetic and copies ran while one was open for 1% -> 0% of each run, Pallas kernels for 34% -> 34%
where the time goes in v2:
time: 71.3 us; the launch traced here: 71.1 us
  Pallas kernels  67.4 us (95%)
  local copies, waits for them, and re-layouts  1.67 us (2%)
  starting transfers between devices  1.39 us (2%)
    pallas_call x1, Pallas kernels, output(): pl.pallas_call(output_kernel, out_shape=jax.ShapeDtypeStruct((rows, width...  25 us
    pallas_call x1, Pallas kernels, attend(): pl.pallas_call(attend_kernel, out_shape=(jax.ShapeDtypeStruct(k_blk.shape...  23.8 us
    pallas_call x1, Pallas kernels, project(): pl.pallas_call(project_kernel, out_shape=(jax.ShapeDtypeStruct((2, 16, 16...  18.6 us
    unnamed x1, local copies, waits for them, and re-layouts  1.67 us
  transfers between devices with their start and end apart: 1, of which 0 were waited for; matrix products, arithmetic and copies ran while one was open for 0% of the time, Pallas kernels for 34%

profile of v2, /device:TPU:0, one launch (start us, length us, event | category | flops | bytes accessed | tf_op | source)
XLA Modules:
  0.0 71.1 jit_solution(6985406027822135670)
XLA Ops:
  0.6 18.6 %project.1 = (bf16[2,16,16,128]{3,2,1,0:T(8,128)(2,1)}, f32[2,16,128]{2,1,0:T(8,128)}, bf16[16,128,256]{2,1,0:T(8,128)(2,1)}, bf16[16,128,256]{2,1,0:T(8,128)(2,1)}) custom-call(s32[128]{0:T(128)} %lens_h.3, bf16[128,1024]{1,0:T(8,128)(2,1)} %x_h.3, f32[1,1024]{1,0:T(1,128)} %bitcast.1, f32[1,128]{1,0:T(1,128)} %constant.2.clone.freq_h, ...), custom_call_target="tpu_custom_call" | custom-call | tf_op jit(solution)/shard_map/project/pallas_call | solution.py:249
  19.2 1.4 %collective-permute-start = (bf16[16,128,256]{2,1,0:T(8,128)(2,1)}, bf16[16,128,256]{2,1,0:T(8,128)(2,1)}, u32[]{:S(2)}, u32[]{:S(2)}) collective-permute-start(bf16[16,128,256]{2,1,0:T(8,128)(2,1)} %get-tuple-element.14), channel_id=1, source_target_pairs={{0,2},{1,3},{2,0},{3,1},{4,6},{5,7},{6,4},{7,5}} | collective-permute-start | bytes 3145736 | tf_op jit(solution)/shard_map/ppermute | solution.py:550
  20.6 23.8 %attend.1 = (bf16[16,4096,128]{2,1,0:T(8,128)(2,1)}, bf16[16,4096,128]{2,1,0:T(8,128)(2,1)}, bf16[2,16,2048]{2,1,0:T(8,128)(2,1)}) custom-call(s32[128]{0:T(128)} %lens_h.3, bf16[2,16,16,128]{3,2,1,0:T(8,128)(2,1)} %get-tuple-element.10.q_h, f32[2,16,128]{2,1,0:T(8,128)} %get-tuple-element.11.kv_h, bf16[16,4096,128]{2,1,0:T(8,128)(2,1)} %k_in.1, ...), custom_call_target="tpu_custom_call" | custom-call | flops 1073741824 | bytes 67108864 | tf_op jit(solution)/shard_map/attend/pallas_call | solution.py:386
  44.5 0.0 collective-permute-done.got_h
  44.5 25.0 %output.1 = bf16[128,1024]{1,0:T(8,128)(2,1)} custom-call(bf16[2,16,2048]{2,1,0:T(8,128)(2,1)} %get-tuple-element.12.att_h, bf16[16,128,256]{2,1,0:T(8,128)(2,1)} %get-tuple-element.13.keep_h, bf16[16,128,256]{2,1,0:T(8,128)(2,1)} %collective-permute-done.got_h, bf16[128,1024]{1,0:T(8,128)(2,1)} %x_h.3, bf16[2048,1024]{1,0:T(8,128)(2,1)} %wo_h.1, ...), custom_call_target="tpu_custom_call" | custom-call | tf_op jit(solution)/shard_map/output/pallas_call | solution.py:524
  69.5 1.7 %copy.17 = bf16[128,1024]{1,0:T(8,128)(2,1)} copy(bf16[128,1024]{1,0:T(8,128)(2,1)} %output.1) | data formatting | bytes 524288
Async XLA Ops:
  19.2 25.3 %collective-permute-start = (bf16[16,128,256]{2,1,0:T(8,128)(2,1)}, bf16[16,128,256]{2,1,0:T(8,128)(2,1)}, u32[]{:S(2)}, u32[]{:S(2)}) collective-permute-start(bf16[16,128,256]{2,1,0:T(8,128)(2,1)} %get-tuple-element.14), channel_id=1, source_target_pairs={{0,2},{1,3},{2,0},{3,1},{4,6},{5,7},{6,4},{7,5}} | collective-permute-start | bytes 3145736 | tf_op jit(solution)/shard_map/ppermute | solution.py:550

commit v3 on v2

--- a/solution.py
+++ b/solution.py
@@ -49,6 +49,8 @@
 
 
 CHUNKS = 8
+EARLY = 1
+LATE = CHUNKS - EARLY
 
 
 def gated(g, u):
@@ -57,12 +59,13 @@
 
 def project_kernel(lens_h, x_h, gamma_h, freq_h, wq_h, wk_h, wv_h, wg_h, wu_h,
                    q_hbm, kv_hbm, keep_hbm, pay_hbm,
-                   lens_ref, freq_ref, q_out, kv_out, keep_out, pay_out, res_sem, keep_sem, x_ref, gamma_ref, x_sem, wq_v, wkv_v, wg_v, wu_v, h_v, st_send, st_recv,
-                   qp, qd, qx, qr, kvp, kvr, qscr, dsend, drecv, own,
-                   wq_sem, wkv_sem, w_sem, st_ssem, st_rsem, qd_ssem, qd_rsem, q_ssem, q_rsem,
-                   kv_ssem, kv_rsem, d_ssem, d_rsem):
+                   lens_ref, freq_ref, q_out, kv_out, keep_out, pay_out, act_out, res_sem, keep_sem, act_sem, x_ref, gamma_ref, x_sem, wq_v, wg_v, wu_v, h_v, st_send, st_recv,
+                   qp, qd, qx, qr, qscr, dsend, drecv, own, xkeep, xsend, xrecv,
+                   wq_sem, w_sem, st_ssem, st_rsem, qd_ssem, qd_rsem, q_ssem, q_rsem,
+                   d_ssem, d_rsem, x_ssem, x_rsem):
     row, col, chip, core = here()
     partner = col + 1 - 2 * core
+    far = (col + 2) % 4
     me = row * 4 + col
     greet()
 
@@ -72,18 +75,17 @@
     freq_cp = pltpu.make_async_copy(freq_h, freq_ref, x_sem.at[3])
     for cp in (x_cp, gamma_cp, lens_cp, freq_cp):
         cp.start()
-    wq_cp = [pltpu.make_async_copy(wq_h.at[:, pl.ds(512 * p, 512)], wq_v.at[p], wq_sem.at[p]) for p in range(4)]
-    kv_cp = [pltpu.make_async_copy(w.at[:, :], wkv_v.at[:, pl.ds(128 * p, 128)], wkv_sem.at[p]) for p, w in enumerate((wk_h, wv_h))]
-    for cp in wq_cp + kv_cp:
+    q_width = wq_h.shape[1]
+    wq_cp = [pltpu.make_async_copy(wq_h, wq_v.at[:, pl.ds(0, q_width)], wq_sem.at[0]),
+             pltpu.make_async_copy(wk_h, wq_v.at[:, pl.ds(q_width, 128)], wq_sem.at[1]),
+             pltpu.make_async_copy(wv_h, wq_v.at[:, pl.ds(q_width + 128, 128)], wq_sem.at[2])]
+    for cp in wq_cp:
         cp.start()
 
     def weight_copies(n):
-        out = []
-        for quarter in range(4):
-            cols = pl.ds(pl.multiple_of(2048 * quarter + 256 * n, 256), 256)
-            out.append(pltpu.make_async_copy(wg_h.at[:, cols], wg_v.at[n, quarter], w_sem.at[n, quarter, 0]))
-            out.append(pltpu.make_async_copy(wu_h.at[:, cols], wu_v.at[n, quarter], w_sem.at[n, quarter, 1]))
-        return out
+        cols = pl.ds(pl.multiple_of(1024 * n, 1024), 1024)
+        return (pltpu.make_async_copy(wg_h.at[:, cols], wg_v.at[n], w_sem.at[n, 0]),
+                pltpu.make_async_copy(wu_h.at[:, cols], wu_v.at[n], w_sem.at[n, 1]))
 
     def start_weights(n, carry):
         for cp in weight_copies(n):
@@ -129,59 +131,59 @@
 
     for cp in wq_cp:
         cp.wait()
-    for p in range(4):
-        part = dot(h_v[...], wq_v[p]).astype(BF16)
+    for lo in range(0, q_width + 256, 512):
+        hi = min(lo + 512, q_width + 256)
+        part = dot(h_v[...], wq_v[:, lo:hi]).astype(BF16)
         for d in range(8):
-            qp[d % 2, d // 2, :, 512 * p:512 * p + 512] = part[16 * d:16 * d + 16]
+            qp[d % 2, d // 2, :, lo:hi] = part[16 * d:16 * d + 16]
     qd_cp = remote(qp.at[1 - core], qd, qd_ssem, qd_rsem, row, partner)
     qd_cp.start()
-    for cp in kv_cp:
-        cp.wait()
-    kvp[...] = dot(h_v[...], wkv_v[...]).reshape(8, 16, 256)
-    kv_sends = []
-    for d in (1, 2, 3):
-        peer = (col + d) % 4
-        cp = remote(kvp.at[row * 4 + peer], kvr.at[d - 1], kv_ssem.at[d - 1], kv_rsem.at[d - 1], row, peer)
-        cp.start()
-        kv_sends.append(cp)
 
     def pair_copy(n):
         return remote(dsend.at[n], drecv.at[n], d_ssem.at[n], d_rsem.at[n], row, partner)
 
-    def compute_chunk(n):
+    def compute_chunk(n, sum_one=None):
         for cp in weight_copies(n):
             cp.wait()
+        if sum_one is not None:
+            pair_copy(n - 2).wait_recv()
+        def products(owner):
+            cols = pl.ds(pl.multiple_of(512 * owner, 512), 512)
+            return dot(h_v[...], wg_v[n, :, cols]), dot(h_v[...], wu_v[n, :, cols])
+
+        theirs, mine = products(1 - core), products(core)
         for xr in range(2):
-            quarter = 2 * xr + (1 - core)
-            dsend[n, xr, 0] = dot(h_v[...], wg_v[n, quarter]).astype(BF16)
-            dsend[n, xr, 1] = dot(h_v[...], wu_v[n, quarter]).astype(BF16)
+            for part in range(2):
+                dsend[n, xr, part] = theirs[part][:, 256 * xr:256 * xr + 256].astype(BF16)
+                own[n % 3, xr, part] = mine[part][:, 256 * xr:256 * xr + 256]
+        started = [] if sum_one is None else sum_one(n - 2)
         pair_copy(n).start()
-        for xr in range(2):
-            quarter = 2 * xr + core
-            own[n % 3, xr, 0] = dot(h_v[...], wg_v[n, quarter])
-            own[n % 3, xr, 1] = dot(h_v[...], wu_v[n, quarter])
+        for cp in started:
+            cp.start()
 
     def sum_chunk(n):
-        pair_copy(n).wait_recv()
         keep = own[n % 3, chip] + drecv[n, chip].astype(F32)
         give = (own[n % 3, 1 - chip] + drecv[n, 1 - chip].astype(F32)).astype(BF16)
         return keep, give
 
+    def far_copy(n):
+        return remote(xsend.at[n], xrecv.at[n], x_ssem.at[n], x_rsem.at[n], row, far)
+
+    def sum_early(n):
+        keep, give = sum_chunk(n)
+        xkeep[n] = keep
+        xsend[n] = give
+        return [far_copy(n)]
+
     def sum_late(n):
         keep, give = sum_chunk(n)
-        for part in range(2):
-            keep_out[part * CHUNKS + n] = keep[part].astype(BF16)
-            pay_out[part * CHUNKS + n] = give[part]
-        for cp in late_copies(n):
-            cp.start()
+        keep_out[n - EARLY] = keep.astype(BF16)
+        pay_out[n - EARLY] = give
+        return late_copies(n - EARLY)
 
     def late_copies(m):
-        out = []
-        for part in range(2):
-            block = part * CHUNKS + m
-            out.append(pltpu.make_async_copy(keep_out.at[block], keep_hbm.at[block], keep_sem.at[block, 0]))
-            out.append(pltpu.make_async_copy(pay_out.at[block], pay_hbm.at[block], keep_sem.at[block, 1]))
-        return out
+        return (pltpu.make_async_copy(keep_out.at[m], keep_hbm.at[m], keep_sem.at[m, 0]),
+                pltpu.make_async_copy(pay_out.at[m], pay_hbm.at[pl.ds(2 * m, 2)], keep_sem.at[m, 1]))
 
     compute_chunk(0)
 
@@ -197,13 +199,20 @@
 
     compute_chunk(1)
 
-    def step(n, carry):
-        compute_chunk(n)
-        sum_late(n - 2)
-        return carry
-
-    lax.fori_loop(2, CHUNKS, step, 0)
-    sum_late(CHUNKS - 2)
+    def step(sum_one):
+        def body(n, carry):
+            compute_chunk(n, sum_one)
+            return carry
+        return body
+
+    def last_sum(n):
+        pair_copy(n).wait_recv()
+        for cp in sum_late(n):
+            cp.start()
+
+    lax.fori_loop(2, EARLY + 2, step(sum_early), 0)
+    lax.fori_loop(EARLY + 2, CHUNKS, step(sum_late), 0)
+    last_sum(CHUNKS - 2)
 
     def rotate(vals):
         return vals * cosv + pltpu.roll(vals, 64, 1) * sinv
@@ -218,21 +227,26 @@
     q_out[...] = qscr[...].astype(BF16)
     q_cp = pltpu.make_async_copy(q_out, q_hbm, res_sem.at[0])
     q_cp.start()
-    for cp in kv_sends:
-        cp.wait_recv()
-    kv = kvp[me] + kvr[0] + kvr[1] + kvr[2]
-    kv_out[0] = rotate(kv[:, :128]).astype(BF16).astype(F32)
-    kv_out[1] = kv[:, 128:].astype(BF16).astype(F32)
-
+    kv_out[0] = rotate(q_same[:, q_width:q_width + 128]).astype(BF16).astype(F32)
+    kv_out[1] = q_same[:, q_width + 128:].astype(BF16).astype(F32)
     kv_cp = pltpu.make_async_copy(kv_out, kv_hbm, res_sem.at[1])
     kv_cp.start()
-    sum_late(CHUNKS - 1)
-    for cp in (q_cp, kv_cp):
+    last_sum(CHUNKS - 1)
+    act_cp = []
+    for n in range(EARLY):
+        far_copy(n).wait_recv()
+        full = xkeep[n] + xrecv[n].astype(F32)
+        act_out[n] = gated(full[0], full[1])
+        cp = pltpu.make_async_copy(act_out.at[n], pay_hbm.at[2 * LATE + n], act_sem.at[n])
+        cp.start()
+        act_cp.append(cp)
+        far_copy(n).wait_send()
+    for cp in act_cp + [q_cp, kv_cp]:
         cp.wait()
-    for m in range(CHUNKS):
+    for m in range(LATE):
         for cp in late_copies(m):
             cp.wait()
-    for cp in st_cp + [qd_cp] + kv_sends + q_sends:
+    for cp in st_cp + [qd_cp] + q_sends:
         cp.wait_send()
 
     def drain(n, carry):
@@ -245,30 +259,30 @@
 def project(lens, x_blk, gamma, freqs, w_query, w_key, w_value, w_gate, w_up):
     rows, width = x_blk.shape
     nc = CHUNKS
+    q_width = w_query.shape[1] + w_key.shape[1] + w_value.shape[1]
     hbm = pl.BlockSpec(memory_space=pl.ANY)
     return pl.pallas_call(
         project_kernel,
         out_shape=(
             jax.ShapeDtypeStruct((2, 16, 16, 128), BF16),
             jax.ShapeDtypeStruct((2, 16, 128), F32),
-            jax.ShapeDtypeStruct((2 * CHUNKS, rows, 256), BF16),
-            jax.ShapeDtypeStruct((2 * CHUNKS, rows, 256), BF16),
+            jax.ShapeDtypeStruct((LATE, 2, rows, 256), BF16),
+            jax.ShapeDtypeStruct((2 * LATE + EARLY, rows, 256), BF16),
         ),
         in_specs=[hbm] * 9,
         out_specs=(hbm,) * 4,
         scratch_shapes=[
             pltpu.SMEM((128,), jnp.int32), VMEM((1, 128), F32), VMEM((2, 16, 16, 128), BF16), VMEM((2, 16, 128), F32),
-            VMEM((2 * CHUNKS, rows, 256), BF16), VMEM((2 * CHUNKS, rows, 256), BF16),
-            DMA((2,)), DMA((2 * CHUNKS, 2)),
+            VMEM((LATE, 2, rows, 256), BF16), VMEM((LATE, 2, rows, 256), BF16), VMEM((EARLY, rows, 256), BF16),
+            DMA((2,)), DMA((LATE, 2)), DMA((EARLY,)),
             VMEM((rows, width), BF16), VMEM((1, width), F32), DMA((4,)),
-            VMEM((4, width, 512), BF16), VMEM((width, 256), BF16),
-            VMEM((nc, 4, width, 256), BF16), VMEM((nc, 4, width, 256), BF16),
+            VMEM((width, q_width), BF16), VMEM((nc, width, 1024), BF16), VMEM((nc, width, 1024), BF16),
             VMEM((rows, width), BF16), VMEM((8, rows), F32), VMEM((3, 8, rows), F32),
-            VMEM((2, 4, 16, 2048), BF16), VMEM((4, 16, 2048), BF16), VMEM((4, 16, 2048), BF16), VMEM((3, 16, 2048), BF16),
-            VMEM((8, 16, 256), F32), VMEM((3, 16, 256), F32), VMEM((2, 16, 16, 128), F32),
+            VMEM((2, 4, 16, q_width), BF16), VMEM((4, 16, q_width), BF16), VMEM((4, 16, q_width), BF16), VMEM((3, 16, q_width), BF16),
+            VMEM((2, 16, 16, 128), F32),
             VMEM((nc, 2, 2, rows, 256), BF16), VMEM((nc, 2, 2, rows, 256), BF16), VMEM((3, 2, 2, rows, 256), F32),
-            DMA((4,)), DMA((2,)), DMA((nc, 4, 2)), DMA((3,)), DMA((3,)), DMA, DMA, DMA((3,)), DMA((3,)),
-            DMA((3,)), DMA((3,)), DMA((nc,)), DMA((nc,)),
+            VMEM((EARLY, 2, rows, 256), F32), VMEM((EARLY, 2, rows, 256), BF16), VMEM((EARLY, 2, rows, 256), BF16),
+            DMA((3,)), DMA((nc, 2)), DMA((3,)), DMA((3,)), DMA, DMA, DMA((3,)), DMA((3,)), DMA((nc,)), DMA((nc,)), DMA((EARLY,)), DMA((EARLY,)),
         ],
         compiler_params=pltpu.CompilerParams(collective_id=0, has_side_effects=True, vmem_limit_bytes=VMEM_ALL),
         name="project",
@@ -404,25 +418,30 @@
     )(lens, q, kv, k_blk, v_blk)
 
 
-HALF = 64
-PIECES = 4
-
-
-def output_kernel(att_h, keep_h, got_h, x_h, wo_h, wd_h, y_hbm,
-                  att_ref, keep_v, got_v, x_ref, y_out, act_v, in_sem, wo_v, wd_v, attf, acc, ysend, yrecv,
+GROUPS = ((0, 64), (64, 96), (96, 128))
+WIDE = 256 * CHUNKS
+EDGES = (0, 256 * EARLY, 256 * (EARLY + 4), WIDE)
+
+
+def output_kernel(att_h, keep_h, pay_h, got_h, x_h, wo_h, wd_h, y_out,
+                  att_ref, keep_v, got_v, x_ref, act_v, in_sem, wo_v, wd_v, attf, acc, ysend, yrecv,
                   wo_sem, wd_sem, a_ssem, a_rsem, f_ssem, f_rsem, g_ssem, g_rsem, h_ssem, h_rsem, c_ssem, c_rsem, y_ssem, y_rsem):
     greet()
     row, col, chip, core = here()
     partner = col + 1 - 2 * core
     far = (col + 2) % 4
-    far_partner = (partner + 2) % 4
-    order = (col, far, partner, far_partner)
-    in_cp = [pltpu.make_async_copy(src, dst, in_sem.at[s]) for s, (src, dst) in enumerate(((att_h, att_ref), (keep_h, keep_v), (got_h, got_v), (x_h, x_ref)))]
+    order = (2 * core + chip, 2 * (1 - core) + chip, 2 * core + 1 - chip, 2 * (1 - core) + 1 - chip)
+    rs = pl.ds(0, 2 * LATE)
+    moves = [(att_h, att_ref), (keep_h, keep_v), (got_h.at[rs], got_v), (x_h, x_ref)]
+    for s, src in ((0, pay_h), (2, got_h)):
+        for n in range(EARLY):
+            moves.append((src.at[2 * LATE + n], act_v.at[:, pl.ds(WIDE * s + 256 * n, 256)]))
+    in_cp = [pltpu.make_async_copy(src, dst, in_sem.at[s]) for s, (src, dst) in enumerate(moves)]
     for cp in in_cp:
         cp.start()
     wd_cp = []
     for s, owner in enumerate(order):
-        wd_cp.append(pltpu.make_async_copy(wd_h.at[pl.ds(pl.multiple_of(owner * 2048, 2048), 2048), :], wd_v.at[s], wd_sem.at[s]))
+        wd_cp.append(pltpu.make_async_copy(wd_h.at[:, owner], wd_v.at[s], wd_sem.at[s]))
     wo_cp = pltpu.make_async_copy(wo_h, wo_v, wo_sem)
 
     in_cp[0].wait()
@@ -440,42 +459,37 @@
     f_own.start()
 
     def piece(s, r, p):
-        return act_v.at[s, r, :, pl.ds(512 * p, 512)]
+        lo, hi = GROUPS[r]
+        return act_v.at[pl.ds(lo, hi - lo), pl.ds(WIDE * s + EDGES[p], EDGES[p + 1] - EDGES[p])]
 
     in_cp[1].wait()
     in_cp[2].wait()
-    for cp in (wd_cp[0], wd_cp[2], wo_cp, wd_cp[1], wd_cp[3]):
-        cp.start()
-    g_cp, h_cp, c_cp = {}, {}, []
-    for r in range(2):
-        rows = slice(HALF * r, HALF * r + HALF)
-        for p in range(PIECES):
-            for n in (2 * p, 2 * p + 1):
-                g = keep_v[n, rows].astype(F32) + got_v[n, rows].astype(F32)
-                u = keep_v[CHUNKS + n, rows].astype(F32) + got_v[CHUNKS + n, rows].astype(F32)
-                act_v[0, r, :, 256 * n:256 * n + 256] = gated(g, u)
-            g_cp[r, p] = remote(piece(0, r, p), piece(1, r, p), g_ssem.at[r, p], g_rsem.at[r, p], row, far)
+    for cp in (wd_cp[0], wd_cp[1], wo_cp, wd_cp[2], wd_cp[3]):
+        cp.start()
+    g_cp, h_cp = {}, {}
+    for r, (lo, hi) in enumerate(GROUPS):
+        rows = slice(lo, hi)
+        for p in (1, 2):
+            for n in range(EDGES[p] // 256 - EARLY, EDGES[p + 1] // 256 - EARLY):
+                g = keep_v[n, 0, rows].astype(F32) + got_v[2 * n, rows].astype(F32)
+                u = keep_v[n, 1, rows].astype(F32) + got_v[2 * n + 1, rows].astype(F32)
+                at = 256 * (EARLY + n)
+                act_v[rows, at:at + 256] = gated(g, u)
+            g_cp[r, p] = remote(piece(0, r, p), piece(2, r, p), g_ssem.at[r, p - 1], g_rsem.at[r, p - 1], row, far)
             g_cp[r, p].start()
-            h_cp[r, p] = remote(piece(1, r, p), piece(3, r, p), h_ssem.at[r, p], h_rsem.at[r, p], row, partner)
-        cp = remote(act_v.at[0, r], act_v.at[2, r], c_ssem.at[r], c_rsem.at[r], row, partner)
-        cp.start()
-        c_cp.append(cp)
-
-    def whole(s):
-        return act_v[s].reshape(2 * HALF, 2048)
-
-    def add(lhs, rhs, first=False):
-        for c in range(2):
-            cols = slice(512 * c, 512 * c + 512)
-            part = dot(lhs, rhs[:, cols])
-            acc[:, cols] = part if first else acc[:, cols] + part
-
-    wd_cp[0].wait()
-    add(whole(0), wd_v.at[0], True)
+            h_cp[r, p] = remote(piece(2, r, p), piece(3, r, p), h_ssem.at[r, p - 1], h_rsem.at[r, p - 1], row, partner)
+    for cp in in_cp[4:]:
+        cp.wait()
+    every = pl.ds(0, 128)
+    first = pl.ds(2 * WIDE, EDGES[1])
+    c_cp = [remote(act_v.at[every, pl.ds(0, WIDE)], act_v.at[every, pl.ds(WIDE, WIDE)], c_ssem.at[0], c_rsem.at[0], row, partner),
+            remote(act_v.at[every, first], act_v.at[every, pl.ds(3 * WIDE, EDGES[1])], c_ssem.at[1], c_rsem.at[1], row, partner)]
     for cp in c_cp:
-        cp.wait_recv()
-    wd_cp[2].wait()
-    add(whole(2), wd_v.at[2])
+        cp.start()
+
+    def down(rows, s, k0, k1):
+        return dot(act_v[rows, WIDE * s + k0:WIDE * s + k1], wd_v[s, k0 // 256:k1 // 256].reshape(k1 - k0, -1))
+
     f_cp = []
     for s, (dy, dx) in enumerate(around):
         a_cp[s].wait_recv()
@@ -483,61 +497,71 @@
         cp = remote(attf.at[index, core], attf.at[index, core], f_ssem.at[s], f_rsem.at[s], row, partner)
         cp.start()
         f_cp.append(cp)
+    for cp in c_cp:
+        cp.wait_recv()
+    wd_cp[0].wait()
+    wd_cp[1].wait()
+    acc[...] = down(slice(0, 128), 0, 0, WIDE) + down(slice(0, 128), 1, 0, WIDE)
     wo_cp.wait()
     for cp in f_cp + [f_own]:
         cp.wait_recv()
-    add(attf[...].reshape(2 * HALF, 2048), wo_v)
-    wd_cp[1].wait()
+    acc[...] += dot(attf[...].reshape(128, 2048), wo_v[...])
+    wd_cp[2].wait()
     wd_cp[3].wait()
     y_cp = {}
-    for r in range(2):
-        rows = slice(HALF * r, HALF * r + HALF)
-        for p in range(PIECES):
+
+    def finish(r, p):
+        lo, hi = GROUPS[r]
+        rows, window = slice(lo, hi), pl.ds(lo, hi - lo)
+        k0, k1 = (0, EDGES[2]) if p == 1 else (EDGES[2], WIDE)
+        h_cp[r, p].wait_recv()
+        part = acc[rows] + (down(rows, 2, k0, k1) + down(rows, 3, k0, k1))
+        if p == 1:
+            acc[rows] = part
+        else:
+            ysend[rows] = part.astype(BF16)
+            y_cp[r] = remote(ysend.at[window], yrecv.at[window], y_ssem.at[r], y_rsem.at[r], 1 - row, col)
+            y_cp[r].start()
+
+    last = None
+    for r in range(len(GROUPS)):
+        for p in (1, 2):
             g_cp[r, p].wait_recv()
             h_cp[r, p].start()
-        for p in range(PIECES):
-            h_cp[r, p].wait_recv()
-        for c in range(2):
-            cols = slice(512 * c, 512 * c + 512)
-            part = dot(act_v[1, r], wd_v[1, :, cols]) + dot(act_v[3, r], wd_v[3, :, cols])
-            ysend[r, c] = (acc[rows, cols] + part).astype(BF16)
-            y_cp[r, c] = remote(ysend.at[r, c], yrecv.at[r, c], y_ssem.at[r, c], y_rsem.at[r, c], 1 - row, col)
-            y_cp[r, c].start()
+            if last is not None:
+                finish(*last)
+            last = (r, p)
+    finish(*last)
     in_cp[3].wait()
-    for r in range(2):
-        rows = slice(HALF * r, HALF * r + HALF)
-        for c in range(2):
-            cols = slice(512 * c, 512 * c + 512)
-            y_cp[r, c].wait_recv()
-            both = ysend[r, c].astype(F32) + yrecv[r, c].astype(F32)
-            y_out[rows, cols] = (x_ref[rows, cols].astype(F32) + both).astype(BF16)
-    res = pltpu.make_async_copy(y_out, y_hbm, in_sem.at[0])
-    res.start()
+    for r, (lo, hi) in enumerate(GROUPS):
+        rows = slice(lo, hi)
+        y_cp[r].wait_recv()
+        both = ysend[rows].astype(F32) + yrecv[rows].astype(F32)
+        y_out[rows] = (x_ref[rows].astype(F32) + both).astype(BF16)
     for cp in a_cp + c_cp + f_cp + [f_own] + list(g_cp.values()) + list(h_cp.values()) + list(y_cp.values()):
         cp.wait_send()
-    res.wait()
-
-
-def output(att, keep, got, x_blk, w_out, w_down):
+
+
+def output(att, keep, pay, got, x_blk, w_out, w_down):
     rows, width = x_blk.shape
     hbm = pl.BlockSpec(memory_space=pl.ANY)
+    groups = len(GROUPS)
     return pl.pallas_call(
         output_kernel,
-        out_shape=jax.ShapeDtypeStruct((rows, width), BF16),
-        in_specs=[hbm] * 6,
-        out_specs=hbm,
+        out_shape=pltpu.VMEM((rows, width), BF16),
+        in_specs=[hbm] * 7,
+        out_specs=pl.BlockSpec(memory_space=VMEM),
         scratch_shapes=[
-            VMEM((2, 16, 2048), BF16), VMEM((2 * CHUNKS, rows, 256), BF16), VMEM((2 * CHUNKS, rows, 256), BF16),
-            VMEM((rows, width), BF16), VMEM((rows, width), BF16),
-            VMEM((4, 2, HALF, 256 * CHUNKS), BF16), DMA((4,)),
-            VMEM((2048, width), BF16), VMEM((4, 2048, width), BF16), VMEM((4, 2, 16, 2048), BF16),
-            VMEM((rows, width), F32), VMEM((2, 2, HALF, 512), BF16), VMEM((2, 2, HALF, 512), BF16),
-            DMA, DMA((4,)), DMA((3,)), DMA((3,)), DMA((4,)), DMA((4,)), DMA((2, PIECES)), DMA((2, PIECES)), DMA((2, PIECES)), DMA((2, PIECES)),
-            DMA((2,)), DMA((2,)), DMA((2, 2)), DMA((2, 2)),
+            VMEM((2, 16, 2048), BF16), VMEM((LATE, 2, rows, 256), BF16), VMEM((2 * LATE, rows, 256), BF16),
+            VMEM((rows, width), BF16), VMEM((rows, 4 * WIDE), BF16), DMA((4 + 2 * EARLY,)),
+            VMEM((2048, width), BF16), VMEM((4, CHUNKS, 256, width), BF16), VMEM((4, 2, 16, 2048), BF16),
+            VMEM((rows, width), F32), VMEM((rows, width), BF16), VMEM((rows, width), BF16),
+            DMA, DMA((4,)), DMA((3,)), DMA((3,)), DMA((4,)), DMA((4,)), DMA((groups, 2)), DMA((groups, 2)), DMA((groups, 2)), DMA((groups, 2)),
+            DMA((2,)), DMA((2,)), DMA((groups,)), DMA((groups,)),
         ],
-        compiler_params=pltpu.CompilerParams(collective_id=1, has_side_effects=True, vmem_limit_bytes=VMEM_ALL),
+        compiler_params=pltpu.CompilerParams(collective_id=1, has_side_effects=True, vmem_limit_bytes=48 * 2 ** 20),
         name="output",
-    )(att, keep, got, x_blk, w_out, w_down)
+    )(*[pltpu.with_memory_space_constraint(v, pltpu.HBM) for v in (att, keep, pay, got, x_blk, w_out, w_down.reshape(CHUNKS, 4, 256, width))])
 
 
 def solution(mesh):
@@ -549,7 +573,7 @@
         q, kv, keep, pay = project(lens, x_blk, gamma[None, :], freqs, w_query, w_key, w_value, w_gate, w_up)
         got = lax.ppermute(pay, "tx", across)
         k_out, v_out, att = attend(lens, q, kv, k_blk, v_blk)
-        y = output(att, keep, got, x_blk, w_out, w_down)
+        y = output(att, keep, pay, got, x_blk, w_out, w_down)
         return y, k_out, v_out
 
     in_specs = (P("dp", "tx"), P("dp"), cache_spec, cache_spec, P("tx"), P("tx", "ty"), P("tx", None), P("tx", None), P("tx", "ty"), P("tx", "ty"), P("ty", "tx"), P("ty", "tx"))

time: 71.3 us -> 67.2 us (0.942)
  Pallas kernels: 67.4 us -> 64.6 us
  local copies, waits for them, and re-layouts: 1.67 us -> 0.71 us
    pallas_call x1, Pallas kernels: 25 us -> 22.3 us  [output(): pl.pallas_call(output_kernel, out_shape=pltpu.VMEM((rows, width), BF16),...]
    unnamed x1, local copies, waits for them, and re-layouts: 1.67 us -> 0.71 us
  transfers between devices with their start and end apart: 1 -> 1, of which waited for: 0 -> 0; matrix products, arithmetic and copies ran while one was open for 0% -> 0% of each run, Pallas kernels for 34% -> 35%
where the time goes in v3:
time: 67.2 us; the launch traced here: 67.1 us
  Pallas kernels  64.6 us (96%)
  starting transfers between devices  1.14 us (2%)
  local copies, waits for them, and re-layouts  0.71 us (1%)
    pallas_call x1, Pallas kernels, attend(): pl.pallas_call(attend_kernel, out_shape=(jax.ShapeDtypeStruct(k_blk.shape...  23.4 us
    pallas_call x1, Pallas kernels, output(): pl.pallas_call(output_kernel, out_shape=pltpu.VMEM((rows, width), BF16),...  22.3 us
    pallas_call x1, Pallas kernels, project(): pl.pallas_call(project_kernel, out_shape=(jax.ShapeDtypeStruct((2, 16, 16...  18.8 us
  transfers between devices with their start and end apart: 1, of which 0 were waited for; matrix products, arithmetic and copies ran while one was open for 0% of the time, Pallas kernels for 35%

profile of v3, /device:TPU:0, one launch (start us, length us, event | category | flops | bytes accessed | tf_op | source)
XLA Modules:
  0.0 67.1 jit_solution(8568078393084535255)
XLA Ops:
  0.6 18.8 %project.1 = (bf16[2,16,16,128]{3,2,1,0:T(8,128)(2,1)}, f32[2,16,128]{2,1,0:T(8,128)}, bf16[7,2,128,256]{3,2,1,0:T(8,128)(2,1)}, bf16[15,128,256]{2,1,0:T(8,128)(2,1)}) custom-call(s32[128]{0:T(128)} %lens_h.3, bf16[128,1024]{1,0:T(8,128)(2,1)} %x_h.3, f32[1,1024]{1,0:T(1,128)} %bitcast.3, f32[1,128]{1,0:T(1,128)} %constant.2.clone.freq_h, ...), custom_call_target="tpu_custom_call" | custom-call | tf_op jit(solution)/shard_map/project/pallas_call | solution.py:264
  19.5 1.1 %collective-permute-start = (bf16[15,128,256]{2,1,0:T(8,128)(2,1)}, bf16[15,128,256]{2,1,0:T(8,128)(2,1)}, u32[]{:S(2)}, u32[]{:S(2)}) collective-permute-start(bf16[15,128,256]{2,1,0:T(8,128)(2,1)} %get-tuple-element.14.pay_h), channel_id=1, source_target_pairs={{0,2},{1,3},{2,0},{3,1},{4,6},{5,7},{6,4},{7,5}} | collective-permute-start | bytes 2949128 | tf_op jit(solution)/shard_map/ppermute | solution.py:574
  20.6 23.4 %attend.1 = (bf16[16,4096,128]{2,1,0:T(8,128)(2,1)}, bf16[16,4096,128]{2,1,0:T(8,128)(2,1)}, bf16[2,16,2048]{2,1,0:T(8,128)(2,1)}) custom-call(s32[128]{0:T(128)} %lens_h.3, bf16[2,16,16,128]{3,2,1,0:T(8,128)(2,1)} %get-tuple-element.10.q_h, f32[2,16,128]{2,1,0:T(8,128)} %get-tuple-element.11.kv_h, bf16[16,4096,128]{2,1,0:T(8,128)(2,1)} %k_in.1, ...), custom_call_target="tpu_custom_call" | custom-call | flops 1073741824 | bytes 67108864 | tf_op jit(solution)/shard_map/attend/pallas_call | solution.py:400
  44.0 0.0 collective-permute-done.got_h
  44.0 22.3 %output.1 = bf16[128,1024]{1,0:T(8,128)(2,1)S(1)} custom-call(bf16[2,16,2048]{2,1,0:T(8,128)(2,1)} %get-tuple-element.12.att_h, bf16[7,2,128,256]{3,2,1,0:T(8,128)(2,1)} %get-tuple-element.13.keep_h, bf16[15,128,256]{2,1,0:T(8,128)(2,1)} %get-tuple-element.14.pay_h, bf16[15,128,256]{2,1,0:T(8,128)(2,1)} %collective-permute-done.got_h, ...), custom_call_target="tpu_custom_call" | custom-call | tf_op jit(solution)/shard_map/output/pallas_call | solution.py:549
  66.4 0.7 %copy.17 = bf16[128,1024]{1,0:T(8,128)(2,1)} copy(bf16[128,1024]{1,0:T(8,128)(2,1)S(1)} %output.1) | data formatting | bytes 524288
Async XLA Ops:
  19.5 24.5 %collective-permute-start = (bf16[15,128,256]{2,1,0:T(8,128)(2,1)}, bf16[15,128,256]{2,1,0:T(8,128)(2,1)}, u32[]{:S(2)}, u32[]{:S(2)}) collective-permute-start(bf16[15,128,256]{2,1,0:T(8,128)(2,1)} %get-tuple-element.14.pay_h), channel_id=1, source_target_pairs={{0,2},{1,3},{2,0},{3,1},{4,6},{5,7},{6,4},{7,5}} | collective-permute-start | bytes 2949128 | tf_op jit(solution)/shard_map/ppermute | solution.py:574

commit v4 on v3

--- a/solution.py
+++ b/solution.py
@@ -44,12 +44,17 @@
         device_id={"ty": ty, "tx": tx}, device_id_type=MESH)
 
 
+def keep_in(space, *arrays):
+    return [pltpu.with_memory_space_constraint(v, space) for v in arrays]
+
+
 def dot(a, b):
     return jnp.dot(a, b, preferred_element_type=F32)
 
 
 CHUNKS = 8
-EARLY = 1
+READY = 5
+EARLY = 2
 LATE = CHUNKS - EARLY
 
 
@@ -57,9 +62,9 @@
     return (jax.nn.silu(g.astype(BF16).astype(F32)) * u.astype(BF16).astype(F32)).astype(BF16)
 
 
-def project_kernel(lens_h, x_h, gamma_h, freq_h, wq_h, wk_h, wv_h, wg_h, wu_h,
-                   q_hbm, kv_hbm, keep_hbm, pay_hbm,
-                   lens_ref, freq_ref, q_out, kv_out, keep_out, pay_out, act_out, res_sem, keep_sem, act_sem, x_ref, gamma_ref, x_sem, wq_v, wg_v, wu_v, h_v, st_send, st_recv,
+def project_kernel(lens_h, x_h, gamma_h, freq_h, wq_h, wk_h, wv_h, wg_h, wu_h, k_h, v_h,
+                   q_out, kv_out, keep_out, pay_out, pre_out,
+                   lens_ref, freq_ref, pre_sem, x_ref, gamma_ref, x_sem, wq_v, wg_v, wu_v, h_v, st_send, st_recv,
                    qp, qd, qx, qr, qscr, dsend, drecv, own, xkeep, xsend, xrecv,
                    wq_sem, w_sem, st_ssem, st_rsem, qd_ssem, qd_rsem, q_ssem, q_rsem,
                    d_ssem, d_rsem, x_ssem, x_rsem):
@@ -178,12 +183,9 @@
     def sum_late(n):
         keep, give = sum_chunk(n)
         keep_out[n - EARLY] = keep.astype(BF16)
-        pay_out[n - EARLY] = give
-        return late_copies(n - EARLY)
-
-    def late_copies(m):
-        return (pltpu.make_async_copy(keep_out.at[m], keep_hbm.at[m], keep_sem.at[m, 0]),
-                pltpu.make_async_copy(pay_out.at[m], pay_hbm.at[pl.ds(2 * m, 2)], keep_sem.at[m, 1]))
+        pay_out[2 * (n - EARLY)] = give[0]
+        pay_out[2 * (n - EARLY) + 1] = give[1]
+        return []
 
     compute_chunk(0)
 
@@ -207,11 +209,17 @@
 
     def last_sum(n):
         pair_copy(n).wait_recv()
-        for cp in sum_late(n):
-            cp.start()
+        sum_late(n)
 
     lax.fori_loop(2, EARLY + 2, step(sum_early), 0)
-    lax.fori_loop(EARLY + 2, CHUNKS, step(sum_late), 0)
+    lax.fori_loop(EARLY + 2, CHUNKS - 1, step(sum_late), 0)
+    pre_cp = []
+    for t in range(READY):
+        for part, src in enumerate((k_h, v_h)):
+            pre_cp.append(pltpu.make_async_copy(src.at[t], pre_out.at[part, t], pre_sem.at[part, t]))
+    for cp in pre_cp:
+        cp.start()
+    lax.fori_loop(CHUNKS - 1, CHUNKS, step(sum_late), 0)
     last_sum(CHUNKS - 2)
 
     def rotate(vals):
@@ -225,27 +233,16 @@
         for head in range(16):
             qscr[half, :, head, :] = rotate(vals[:, 128 * head:128 * head + 128])
     q_out[...] = qscr[...].astype(BF16)
-    q_cp = pltpu.make_async_copy(q_out, q_hbm, res_sem.at[0])
-    q_cp.start()
     kv_out[0] = rotate(q_same[:, q_width:q_width + 128]).astype(BF16).astype(F32)
     kv_out[1] = q_same[:, q_width + 128:].astype(BF16).astype(F32)
-    kv_cp = pltpu.make_async_copy(kv_out, kv_hbm, res_sem.at[1])
-    kv_cp.start()
     last_sum(CHUNKS - 1)
-    act_cp = []
     for n in range(EARLY):
         far_copy(n).wait_recv()
         full = xkeep[n] + xrecv[n].astype(F32)
-        act_out[n] = gated(full[0], full[1])
-        cp = pltpu.make_async_copy(act_out.at[n], pay_hbm.at[2 * LATE + n], act_sem.at[n])
-        cp.start()
-        act_cp.append(cp)
+        pay_out[2 * LATE + n] = gated(full[0], full[1])
         far_copy(n).wait_send()
-    for cp in act_cp + [q_cp, kv_cp]:
+    for cp in pre_cp:
         cp.wait()
-    for m in range(LATE):
-        for cp in late_copies(m):
-            cp.wait()
     for cp in st_cp + [qd_cp] + q_sends:
         cp.wait_send()
 
@@ -256,7 +253,7 @@
     lax.fori_loop(0, CHUNKS, drain, 0)
 
 
-def project(lens, x_blk, gamma, freqs, w_query, w_key, w_value, w_gate, w_up):
+def project(lens, x_blk, gamma, freqs, w_query, w_key, w_value, w_gate, w_up, k_blk, v_blk):
     rows, width = x_blk.shape
     nc = CHUNKS
     q_width = w_query.shape[1] + w_key.shape[1] + w_value.shape[1]
@@ -264,17 +261,16 @@
     return pl.pallas_call(
         project_kernel,
         out_shape=(
-            jax.ShapeDtypeStruct((2, 16, 16, 128), BF16),
-            jax.ShapeDtypeStruct((2, 16, 128), F32),
-            jax.ShapeDtypeStruct((LATE, 2, rows, 256), BF16),
-            jax.ShapeDtypeStruct((2 * LATE + EARLY, rows, 256), BF16),
+            VMEM((2, 16, 16, 128), BF16),
+            VMEM((2, 16, 128), F32),
+            VMEM((LATE, 2, rows, 256), BF16),
+            VMEM((2 * LATE + EARLY, rows, 256), BF16),
+            VMEM((2, READY, *k_blk.shape[1:]), BF16),
         ),
-        in_specs=[hbm] * 9,
-        out_specs=(hbm,) * 4,
+        in_specs=[hbm] * 11,
+        out_specs=(pl.BlockSpec(memory_space=VMEM),) * 5,
         scratch_shapes=[
-            pltpu.SMEM((128,), jnp.int32), VMEM((1, 128), F32), VMEM((2, 16, 16, 128), BF16), VMEM((2, 16, 128), F32),
-            VMEM((LATE, 2, rows, 256), BF16), VMEM((LATE, 2, rows, 256), BF16), VMEM((EARLY, rows, 256), BF16),
-            DMA((2,)), DMA((LATE, 2)), DMA((EARLY,)),
+            pltpu.SMEM((128,), jnp.int32), VMEM((1, 128), F32), DMA((2, READY)),
             VMEM((rows, width), BF16), VMEM((1, width), F32), DMA((4,)),
             VMEM((width, q_width), BF16), VMEM((nc, width, 1024), BF16), VMEM((nc, width, 1024), BF16),
             VMEM((rows, width), BF16), VMEM((8, rows), F32), VMEM((3, 8, rows), F32),
@@ -284,9 +280,9 @@
             VMEM((EARLY, 2, rows, 256), F32), VMEM((EARLY, 2, rows, 256), BF16), VMEM((EARLY, 2, rows, 256), BF16),
             DMA((3,)), DMA((nc, 2)), DMA((3,)), DMA((3,)), DMA, DMA, DMA((3,)), DMA((3,)), DMA((nc,)), DMA((nc,)), DMA((EARLY,)), DMA((EARLY,)),
         ],
-        compiler_params=pltpu.CompilerParams(collective_id=0, has_side_effects=True, vmem_limit_bytes=VMEM_ALL),
+        compiler_params=pltpu.CompilerParams(collective_id=0, has_side_effects=True, vmem_limit_bytes=47 * 2 ** 20),
         name="project",
-    )(lens, x_blk, gamma, freqs, w_query, w_key, w_value, w_gate, w_up)
+    )(*keep_in(pltpu.HBM, lens, x_blk, gamma, freqs, w_query, w_key, w_value, w_gate, w_up, k_blk, v_blk))
 
 
 SLOTS = 12
@@ -294,8 +290,8 @@
 BLOCK = 1024
 
 
-def attend_kernel(lens_h, q_h, kv_h, k_in, v_in, k_out, v_out, att_hbm,
-                  kbuf, vbuf, s_scr, in_sem, out_sem, att_out, lens_ref, q_ref, kv_ref, o_scr, small_sem):
+def attend_kernel(lens_h, q_ref, kv_ref, pre_ref, k_in, v_in, k_out, v_out, att_out,
+                  kbuf, vbuf, s_scr, in_sem, out_sem, lens_ref, o_scr, small_sem):
     row, col, _, _ = here()
     base = (row * 4 + col) * 16
     count, ctx, _ = k_in.shape
@@ -310,14 +306,21 @@
         return (pltpu.make_async_copy(kbuf.at[slot], k_out.at[t], out_sem.at[slot, 0]),
                 pltpu.make_async_copy(vbuf.at[slot], v_out.at[t], out_sem.at[slot, 1]))
 
-    small = [pltpu.make_async_copy(src, dst, small_sem.at[s]) for s, (src, dst) in enumerate(((lens_h, lens_ref), (q_h, q_ref), (kv_h, kv_ref)))]
-    for cp in small:
-        cp.start()
-    for t in range(min(AHEAD, count)):
+    lens_cp = pltpu.make_async_copy(lens_h, lens_ref, small_sem)
+    lens_cp.start()
+    for t in range(READY, AHEAD):
         for cp in in_copies(t):
             cp.start()
-    for cp in small:
-        cp.wait()
+    lens_cp.wait()
+
+    def take(t, slot):
+        def move(b, carry):
+            rows = pl.ds(pl.multiple_of(b * 512, 512), 512)
+            kbuf[slot, rows] = pre_ref[0, t, rows]
+            vbuf[slot, rows] = pre_ref[1, t, rows]
+            return carry
+
+        lax.fori_loop(0, ctx // 512, move, 0)
 
     def attend(t, slot, length, blocks):
         q = jnp.concatenate([q_ref[0, t], q_ref[1, t]], axis=0)
@@ -351,8 +354,15 @@
 
     def body(t, carry):
         slot = lax.rem(t, SLOTS)
-        for cp in in_copies(t):
-            cp.wait()
+        @pl.when(t < READY)
+        def _():
+            take(t, slot)
+
+        @pl.when(t >= READY)
+        def _():
+            for cp in in_copies(t):
+                cp.wait()
+
         length = lens_ref[base + t]
         start = pl.multiple_of((length // 16) * 16, 16)
         at_row = lax.broadcasted_iota(jnp.int32, (16, 128), 0) == length - start
@@ -385,66 +395,58 @@
 
     for head in range(32):
         att_out[head // 16, :, 128 * (head % 16):128 * (head % 16) + 128] = o_scr[:, head, :].astype(BF16)
-    res = pltpu.make_async_copy(att_out, att_hbm, small_sem.at[3])
-    res.start()
     done_in_loop = max(0, count - AHEAD - (SLOTS - AHEAD)) if count > AHEAD else 0
     for t in range(done_in_loop, count):
         for cp in out_copies(t):
             cp.wait()
-    res.wait()
-
-
-def attend(lens, q, kv, k_blk, v_blk):
+
+
+def attend(lens, q, kv, pre, k_blk, v_blk):
     hbm = pl.BlockSpec(memory_space=pltpu.HBM)
+    vm = pl.BlockSpec(memory_space=VMEM)
     count, ctx, dim = k_blk.shape
     return pl.pallas_call(
         attend_kernel,
         out_shape=(
             jax.ShapeDtypeStruct(k_blk.shape, BF16),
             jax.ShapeDtypeStruct(v_blk.shape, BF16),
-            jax.ShapeDtypeStruct((2, count, 2048), BF16),
+            VMEM((2, count, 2048), BF16),
         ),
-        in_specs=[hbm] * 5,
-        out_specs=(hbm,) * 3,
+        in_specs=[hbm, vm, vm, vm, hbm, hbm],
+        out_specs=(hbm, hbm, vm),
         scratch_shapes=[
             VMEM((SLOTS, ctx, dim), BF16), VMEM((SLOTS, ctx, dim), BF16),
-            VMEM((32, ctx), F32), DMA((SLOTS, 2)), DMA((SLOTS, 2)), VMEM((2, count, 2048), BF16),
-            pltpu.SMEM((128,), jnp.int32), VMEM((2, 16, 16, 128), BF16), VMEM((2, 16, 128), F32),
-            VMEM((count, 32, dim), F32), DMA((4,)),
+            VMEM((32, ctx), F32), DMA((SLOTS, 2)), DMA((SLOTS, 2)),
+            pltpu.SMEM((128,), jnp.int32), VMEM((count, 32, dim), F32), DMA,
         ],
         cost_estimate=pl.CostEstimate(flops=count * 32 * ctx * dim * 4, bytes_accessed=count * ctx * dim * 8, transcendentals=count * 32 * ctx),
-        compiler_params=pltpu.CompilerParams(vmem_limit_bytes=VMEM_ALL),
+        compiler_params=pltpu.CompilerParams(vmem_limit_bytes=30 * 2 ** 20),
         name="attend",
-    )(lens, q, kv, k_blk, v_blk)
-
-
-GROUPS = ((0, 64), (64, 96), (96, 128))
+    )(*keep_in(pltpu.HBM, lens), *keep_in(VMEM, q, kv, pre), *keep_in(pltpu.HBM, k_blk, v_blk))
+
+
 WIDE = 256 * CHUNKS
-EDGES = (0, 256 * EARLY, 256 * (EARLY + 4), WIDE)
-
-
-def output_kernel(att_h, keep_h, pay_h, got_h, x_h, wo_h, wd_h, y_out,
-                  att_ref, keep_v, got_v, x_ref, act_v, in_sem, wo_v, wd_v, attf, acc, ysend, yrecv,
+EDGE = 256 * (EARLY + 4)
+ITEMS = ((0, 64, False), (0, 64, True), (64, 96, False), (64, 96, True), (96, 128, False), (96, 128, True))
+
+
+def output_kernel(att_ref, keep_v, pay_v, got_v, x_h, wo_h, wd_h, y_out,
+                  x_ref, act_v, in_sem, wo_v, wd_v, attf, acc, ysend, yrecv,
                   wo_sem, wd_sem, a_ssem, a_rsem, f_ssem, f_rsem, g_ssem, g_rsem, h_ssem, h_rsem, c_ssem, c_rsem, y_ssem, y_rsem):
     greet()
     row, col, chip, core = here()
     partner = col + 1 - 2 * core
     far = (col + 2) % 4
     order = (2 * core + chip, 2 * (1 - core) + chip, 2 * core + 1 - chip, 2 * (1 - core) + 1 - chip)
-    rs = pl.ds(0, 2 * LATE)
-    moves = [(att_h, att_ref), (keep_h, keep_v), (got_h.at[rs], got_v), (x_h, x_ref)]
-    for s, src in ((0, pay_h), (2, got_h)):
-        for n in range(EARLY):
-            moves.append((src.at[2 * LATE + n], act_v.at[:, pl.ds(WIDE * s + 256 * n, 256)]))
-    in_cp = [pltpu.make_async_copy(src, dst, in_sem.at[s]) for s, (src, dst) in enumerate(moves)]
-    for cp in in_cp:
-        cp.start()
+    x_cp = pltpu.make_async_copy(x_h, x_ref, in_sem)
+    x_cp.start()
     wd_cp = []
     for s, owner in enumerate(order):
         wd_cp.append(pltpu.make_async_copy(wd_h.at[:, owner], wd_v.at[s], wd_sem.at[s]))
     wo_cp = pltpu.make_async_copy(wo_h, wo_v, wo_sem)
 
-    in_cp[0].wait()
+    for cp in (wd_cp[0], wd_cp[1], wo_cp, wd_cp[2], wd_cp[3]):
+        cp.start()
     greeted()
     mine = row * 2 + chip
     around = ((0, 1), (1, 0), (1, 1))
@@ -458,38 +460,40 @@
     f_own = remote(attf.at[mine, core], attf.at[mine, core], f_ssem.at[3], f_rsem.at[3], row, partner)
     f_own.start()
 
-    def piece(s, r, p):
-        lo, hi = GROUPS[r]
-        return act_v.at[pl.ds(lo, hi - lo), pl.ds(WIDE * s + EDGES[p], EDGES[p + 1] - EDGES[p])]
-
-    in_cp[1].wait()
-    in_cp[2].wait()
-    for cp in (wd_cp[0], wd_cp[1], wo_cp, wd_cp[2], wd_cp[3]):
-        cp.start()
-    g_cp, h_cp = {}, {}
-    for r, (lo, hi) in enumerate(GROUPS):
+    def piece(s, item):
+        lo, hi, last = ITEMS[item]
+        c0, c1 = (EDGE, WIDE) if last else (256 * EARLY, EDGE)
+        return act_v.at[pl.ds(lo, hi - lo), pl.ds(WIDE * s + c0, c1 - c0)]
+
+    g_cp, h_cp = [], []
+    for item, (lo, hi, last) in enumerate(ITEMS):
         rows = slice(lo, hi)
-        for p in (1, 2):
-            for n in range(EDGES[p] // 256 - EARLY, EDGES[p + 1] // 256 - EARLY):
-                g = keep_v[n, 0, rows].astype(F32) + got_v[2 * n, rows].astype(F32)
-                u = keep_v[n, 1, rows].astype(F32) + got_v[2 * n + 1, rows].astype(F32)
-                at = 256 * (EARLY + n)
-                act_v[rows, at:at + 256] = gated(g, u)
-            g_cp[r, p] = remote(piece(0, r, p), piece(2, r, p), g_ssem.at[r, p - 1], g_rsem.at[r, p - 1], row, far)
-            g_cp[r, p].start()
-            h_cp[r, p] = remote(piece(2, r, p), piece(3, r, p), h_ssem.at[r, p - 1], h_rsem.at[r, p - 1], row, partner)
-    for cp in in_cp[4:]:
-        cp.wait()
+        for n in range(4, LATE) if last else range(4):
+            g = keep_v[n, 0, rows].astype(F32) + got_v[2 * n, rows].astype(F32)
+            u = keep_v[n, 1, rows].astype(F32) + got_v[2 * n + 1, rows].astype(F32)
+            at = 256 * (EARLY + n)
+            act_v[rows, at:at + 256] = gated(g, u)
+        g_cp.append(remote(piece(0, item), piece(2, item), g_ssem.at[item], g_rsem.at[item], row, far))
+        g_cp[item].start()
+        h_cp.append(remote(piece(2, item), piece(3, item), h_ssem.at[item], h_rsem.at[item], row, partner))
+    for s, src in ((0, pay_v), (2, got_v)):
+        for n in range(EARLY):
+            act_v[:, WIDE * s + 256 * n:WIDE * s + 256 * n + 256] = src[2 * LATE + n]
     every = pl.ds(0, 128)
-    first = pl.ds(2 * WIDE, EDGES[1])
+    first = pl.ds(2 * WIDE, 256 * EARLY)
     c_cp = [remote(act_v.at[every, pl.ds(0, WIDE)], act_v.at[every, pl.ds(WIDE, WIDE)], c_ssem.at[0], c_rsem.at[0], row, partner),
-            remote(act_v.at[every, first], act_v.at[every, pl.ds(3 * WIDE, EDGES[1])], c_ssem.at[1], c_rsem.at[1], row, partner)]
+            remote(act_v.at[every, first], act_v.at[every, pl.ds(3 * WIDE, 256 * EARLY)], c_ssem.at[1], c_rsem.at[1], row, partner)]
     for cp in c_cp:
         cp.start()
 
     def down(rows, s, k0, k1):
         return dot(act_v[rows, WIDE * s + k0:WIDE * s + k1], wd_v[s, k0 // 256:k1 // 256].reshape(k1 - k0, -1))
 
+    for cp in c_cp:
+        cp.wait_recv()
+    wd_cp[0].wait()
+    wd_cp[1].wait()
+    acc[...] = down(slice(0, 128), 0, 0, WIDE) + down(slice(0, 128), 1, 0, WIDE)
     f_cp = []
     for s, (dy, dx) in enumerate(around):
         a_cp[s].wait_recv()
@@ -497,71 +501,67 @@
         cp = remote(attf.at[index, core], attf.at[index, core], f_ssem.at[s], f_rsem.at[s], row, partner)
         cp.start()
         f_cp.append(cp)
-    for cp in c_cp:
+    def attention_part():
+        wo_cp.wait()
+        for cp in f_cp + [f_own]:
+            cp.wait_recv()
+        acc[...] += dot(attf[...].reshape(128, 2048), wo_v[...])
+        wd_cp[2].wait()
+        wd_cp[3].wait()
+
+    y_cp = []
+
+    def finish(item):
+        lo, hi, last = ITEMS[item]
+        rows, window = slice(lo, hi), pl.ds(lo, hi - lo)
+        k0, k1 = (EDGE, WIDE) if last else (0, EDGE)
+        h_cp[item].wait_recv()
+        part = acc[rows] + (down(rows, 2, k0, k1) + down(rows, 3, k0, k1))
+        if last:
+            ysend[rows] = part.astype(BF16)
+            cp = remote(ysend.at[window], yrecv.at[window], y_ssem.at[item], y_rsem.at[item], 1 - row, col)
+            cp.start()
+            y_cp.append((rows, cp))
+        else:
+            acc[rows] = part
+
+    for item in range(len(ITEMS)):
+        g_cp[item].wait_recv()
+        h_cp[item].start()
+        if item:
+            finish(item - 1)
+        else:
+            attention_part()
+    finish(len(ITEMS) - 1)
+    x_cp.wait()
+    for rows, cp in y_cp:
         cp.wait_recv()
-    wd_cp[0].wait()
-    wd_cp[1].wait()
-    acc[...] = down(slice(0, 128), 0, 0, WIDE) + down(slice(0, 128), 1, 0, WIDE)
-    wo_cp.wait()
-    for cp in f_cp + [f_own]:
-        cp.wait_recv()
-    acc[...] += dot(attf[...].reshape(128, 2048), wo_v[...])
-    wd_cp[2].wait()
-    wd_cp[3].wait()
-    y_cp = {}
-
-    def finish(r, p):
-        lo, hi = GROUPS[r]
-        rows, window = slice(lo, hi), pl.ds(lo, hi - lo)
-        k0, k1 = (0, EDGES[2]) if p == 1 else (EDGES[2], WIDE)
-        h_cp[r, p].wait_recv()
-        part = acc[rows] + (down(rows, 2, k0, k1) + down(rows, 3, k0, k1))
-        if p == 1:
-            acc[rows] = part
-        else:
-            ysend[rows] = part.astype(BF16)
-            y_cp[r] = remote(ysend.at[window], yrecv.at[window], y_ssem.at[r], y_rsem.at[r], 1 - row, col)
-            y_cp[r].start()
-
-    last = None
-    for r in range(len(GROUPS)):
-        for p in (1, 2):
-            g_cp[r, p].wait_recv()
-            h_cp[r, p].start()
-            if last is not None:
-                finish(*last)
-            last = (r, p)
-    finish(*last)
-    in_cp[3].wait()
-    for r, (lo, hi) in enumerate(GROUPS):
-        rows = slice(lo, hi)
-        y_cp[r].wait_recv()
         both = ysend[rows].astype(F32) + yrecv[rows].astype(F32)
         y_out[rows] = (x_ref[rows].astype(F32) + both).astype(BF16)
-    for cp in a_cp + c_cp + f_cp + [f_own] + list(g_cp.values()) + list(h_cp.values()) + list(y_cp.values()):
+    for cp in a_cp + c_cp + f_cp + [f_own] + g_cp + h_cp + [cp for _, cp in y_cp]:
         cp.wait_send()
 
 
 def output(att, keep, pay, got, x_blk, w_out, w_down):
     rows, width = x_blk.shape
     hbm = pl.BlockSpec(memory_space=pl.ANY)
-    groups = len(GROUPS)
+    vm = pl.BlockSpec(memory_space=VMEM)
+    items = len(ITEMS)
     return pl.pallas_call(
         output_kernel,
         out_shape=pltpu.VMEM((rows, width), BF16),
-        in_specs=[hbm] * 7,
-        out_specs=pl.BlockSpec(memory_space=VMEM),
+        in_specs=[vm] * 4 + [hbm] * 3,
+        out_specs=vm,
         scratch_shapes=[
-            VMEM((2, 16, 2048), BF16), VMEM((LATE, 2, rows, 256), BF16), VMEM((2 * LATE, rows, 256), BF16),
-            VMEM((rows, width), BF16), VMEM((rows, 4 * WIDE), BF16), DMA((4 + 2 * EARLY,)),
+            VMEM((rows, width), BF16), VMEM((rows, 4 * WIDE), BF16), DMA,
             VMEM((2048, width), BF16), VMEM((4, CHUNKS, 256, width), BF16), VMEM((4, 2, 16, 2048), BF16),
             VMEM((rows, width), F32), VMEM((rows, width), BF16), VMEM((rows, width), BF16),
-            DMA, DMA((4,)), DMA((3,)), DMA((3,)), DMA((4,)), DMA((4,)), DMA((groups, 2)), DMA((groups, 2)), DMA((groups, 2)), DMA((groups, 2)),
-            DMA((2,)), DMA((2,)), DMA((groups,)), DMA((groups,)),
+            DMA, DMA((4,)), DMA((3,)), DMA((3,)), DMA((4,)), DMA((4,)), DMA((items,)), DMA((items,)), DMA((items,)), DMA((items,)),
+            DMA((2,)), DMA((2,)), DMA((items,)), DMA((items,)),
         ],
-        compiler_params=pltpu.CompilerParams(collective_id=1, has_side_effects=True, vmem_limit_bytes=48 * 2 ** 20),
+        compiler_params=pltpu.CompilerParams(collective_id=1, has_side_effects=True, vmem_limit_bytes=32 * 2 ** 20),
         name="output",
-    )(*[pltpu.with_memory_space_constraint(v, pltpu.HBM) for v in (att, keep, pay, got, x_blk, w_out, w_down.reshape(CHUNKS, 4, 256, width))])
+    )(*keep_in(VMEM, att, keep, pay, got), *keep_in(pltpu.HBM, x_blk, w_out, w_down.reshape(CHUNKS, 4, 256, width)))
 
 
 def solution(mesh):
@@ -570,9 +570,9 @@
 
     def layer_shard(x_blk, lens, k_blk, v_blk, gamma, w_query, w_key, w_value, w_gate, w_up, w_out, w_down):
         freqs = np.tile(np.float32(ROPE_BASE ** (-np.arange(0, 128, 2) / 128.0)), 2)[None, :]
-        q, kv, keep, pay = project(lens, x_blk, gamma[None, :], freqs, w_query, w_key, w_value, w_gate, w_up)
+        q, kv, keep, pay, pre = project(lens, x_blk, gamma[None, :], freqs, w_query, w_key, w_value, w_gate, w_up, k_blk, v_blk)
         got = lax.ppermute(pay, "tx", across)
-        k_out, v_out, att = attend(lens, q, kv, k_blk, v_blk)
+        k_out, v_out, att = attend(lens, q, kv, pre, k_blk, v_blk)
         y = output(att, keep, pay, got, x_blk, w_out, w_down)
         return y, k_out, v_out
 

time: 67.2 us -> 65.5 us (0.975)
  Pallas kernels: 64.6 us -> 61.4 us
  waiting for transfers between devices: 0.01 us -> 2.05 us
    pallas_call x1, Pallas kernels: 23.4 us -> 19.4 us  [attend(): pl.pallas_call(attend_kernel, out_shape=(jax.ShapeDtypeStruct(k_blk.shape...]
    pallas_call x1, Pallas kernels: 18.8 us -> 20.9 us  [project(): pl.pallas_call(project_kernel, out_shape=(VMEM((2, 16, 16, 128), BF16), V...]
    ppermute x1, waiting for transfers between devices: 0.01 us -> 2.05 us  [layer_shard(): got = lax.ppermute(pay, 'tx', across)]
    pallas_call x1, Pallas kernels: 22.3 us -> 21 us  [output(): pl.pallas_call(output_kernel, out_shape=pltpu.VMEM((rows, width), BF16),...]
  transfers between devices with their start and end apart: 1 -> 1, of which waited for: 0 -> 1; matrix products, arithmetic and copies ran while one was open for 0% -> 0% of each run, Pallas kernels for 35% -> 30%
where the time goes in v4:
time: 65.5 us; the launch traced here: 65.4 us
  Pallas kernels  61.4 us (94%)
  waiting for transfers between devices  2.05 us (3%)
  local copies, waits for them, and re-layouts  0.71 us (1%)
  between operations  0.66 us (1%)
    pallas_call x1, Pallas kernels, output(): pl.pallas_call(output_kernel, out_shape=pltpu.VMEM((rows, width), BF16),...  21 us
    pallas_call x1, Pallas kernels, project(): pl.pallas_call(project_kernel, out_shape=(VMEM((2, 16, 16, 128), BF16), V...  20.9 us
    pallas_call x1, Pallas kernels, attend(): pl.pallas_call(attend_kernel, out_shape=(jax.ShapeDtypeStruct(k_blk.shape...  19.4 us
    ppermute x1, waiting for transfers between devices, layer_shard(): got = lax.ppermute(pay, 'tx', across)  2.05 us
  transfers between devices with their start and end apart: 1, of which 1 were waited for; matrix products, arithmetic and copies ran while one was open for 0% of the time, Pallas kernels for 30%

profile of v4, /device:TPU:0, one launch (start us, length us, event | category | flops | bytes accessed | tf_op | source)
XLA Modules:
  0.0 65.4 jit_solution(6228718065940376457)
XLA Ops:
  0.6 20.9 %project.1 = (bf16[2,16,16,128]{3,2,1,0:T(8,128)(2,1)S(1)}, f32[2,16,128]{2,1,0:T(8,128)S(1)}, bf16[6,2,128,256]{3,2,1,0:T(8,128)(2,1)S(1)}, bf16[14,128,256]{2,...) custom-call(s32[128]{0:T(128)} %lens_h.3, bf16[128,1024]{1,0:T(8,128)(2,1)} %x_h.3, f32[1,1024]{1,0:T(1,128)} %bitcast.3, ...), custom_call_target="tpu_custom_call" | custom-call | tf_op jit(solution)/shard_map/project/pallas_call | solution.py:261
  21.6 0.6 collective-permute-start
  22.2 19.4 %attend.1 = (bf16[16,4096,128]{2,1,0:T(8,128)(2,1)}, bf16[16,4096,128]{2,1,0:T(8,128)(2,1)}, bf16[2,16,2048]{2,1,0:T(8,128)(2,1)S(1)}) custom-call(s32[128]{0:T(128)} %lens_h.3, bf16[2,16,16,128]{3,2,1,0:T(8,128)(2,1)S(1)} %get-tuple-element.11.q_ref, f32[2,16,128]{2,1,0:T(8,128)S(1)} %get-tuple-element.12.kv_ref, ...), custom_call_target="tpu_custom_call" | custom-call | flops 1073741824 | bytes 67108864 | tf_op jit(solution)/shard_map/attend/pallas_call | solution.py:408
  41.6 2.0 %collective-permute-done.got_v = bf16[14,128,256]{2,1,0:T(8,128)(2,1)S(1)} collective-permute-done((bf16[14,128,256]{2,1,0:T(8,128)(2,1)S(1)}, bf16[14,128,256]{2,1,0:T(8,128)(2,1)S(1)}, u32[]{:S(2)}, u32[]{:S(2)}) %collective-permute-start) | collective-permute-done | bytes 917536 | tf_op jit(solution)/shard_map/ppermute | solution.py:574
  43.7 21.0 %output.1 = bf16[128,1024]{1,0:T(8,128)(2,1)S(1)} custom-call(bf16[2,16,2048]{2,1,0:T(8,128)(2,1)S(1)} %get-tuple-element.14.att_ref, bf16[6,2,128,256]{3,2,1,0:T(8,128)(2,1)S(1)} %get-tuple-element.15.keep_v, bf16[14,128,256]{2,1,0:T(8,128)(2,1)S(1)} %get-tuple-element.16.pay_v, bf16[14,128,256]{2,1,0:T(8,128)(2,1)S(1)} %collective-permute-done.got_v, ...), custom_call_target="tpu_custom_call" | custom-call | tf_op jit(solution)/shard_map/output/pallas_call | solution.py:550
  64.7 0.7 %copy.17 = bf16[128,1024]{1,0:T(8,128)(2,1)} copy(bf16[128,1024]{1,0:T(8,128)(2,1)S(1)} %output.1) | data formatting | bytes 524288
Async XLA Ops:
  21.6 22.1 %collective-permute-start = (bf16[14,128,256]{2,1,0:T(8,128)(2,1)S(1)}, bf16[14,128,256]{2,1,0:T(8,128)(2,1)S(1)}, u32[]{:S(2)}, u32[]{:S(2)}) collective-permute-start(bf16[14,128,256]{2,1,0:T(8,128)(2,1)S(1)} %get-tuple-element.16.pay_v), channel_id=1, source_target_pairs={{0,2},{1,3},{2,0},{3,1},{4,6},{5,7},{6,4},{7,5}} | collective-permute-start | bytes 2752520 | tf_op jit(solution)/shard_map/ppermute | solution.py:574

commit v5 on v4

--- a/solution.py
+++ b/solution.py
@@ -25,17 +25,20 @@
     return row, col, col // 2, col % 2
 
 
-def greet():
-    row, col, _, _ = here()
-    me = row * 4 + col
+def greet(offsets):
+    row, _, chip, core = here()
     barrier = pltpu.get_barrier_semaphore()
-    for step in range(1, 8):
-        peer = (me + step) % 8
-        pl.semaphore_signal(barrier, inc=1, device_id={"ty": peer // 4, "tx": peer % 4}, device_id_type=MESH)
-
-
-def greeted():
-    pl.semaphore_wait(pltpu.get_barrier_semaphore(), 7)
+    for dy, dx, dc in offsets:
+        peer = {"ty": (row + dy) % 2, "tx": ((chip + dx) % 2) * 2 + (core + dc) % 2}
+        pl.semaphore_signal(barrier, inc=1, device_id=peer, device_id_type=MESH)
+
+
+def greeted(offsets):
+    pl.semaphore_wait(pltpu.get_barrier_semaphore(), len(offsets))
+
+
+MET_EARLY = ((0, 0, 1), (0, 1, 0), (0, 1, 1), (1, 0, 0), (1, 1, 0))
+MET_LATE = ((0, 0, 1), (0, 1, 0), (1, 0, 0), (1, 1, 0))
 
 
 def remote(src, dst, send_sem, recv_sem, ty, tx):
@@ -72,7 +75,7 @@
     partner = col + 1 - 2 * core
     far = (col + 2) % 4
     me = row * 4 + col
-    greet()
+    greet(MET_EARLY)
 
     x_cp = pltpu.make_async_copy(x_h, x_ref, x_sem.at[0])
     gamma_cp = pltpu.make_async_copy(gamma_h, gamma_ref, x_sem.at[1])
@@ -109,7 +112,7 @@
     line2 = jnp.sum(jnp.where(eye, sum2, 0.0), axis=0, keepdims=True)
     first = lax.broadcasted_iota(jnp.int32, (8, rows), 0) == 0
     st_send[...] = jnp.where(first, line1, line2)
-    greeted()
+    greeted(MET_EARLY)
     st_cp = [remote(st_send, st_recv.at[d - 1], st_ssem.at[d - 1], st_rsem.at[d - 1], row, (col + d) % 4) for d in (1, 2, 3)]
     for cp in st_cp:
         cp.start()
@@ -136,13 +139,15 @@
 
     for cp in wq_cp:
         cp.wait()
-    for lo in range(0, q_width + 256, 512):
-        hi = min(lo + 512, q_width + 256)
+    q_parts = ((0, 1024), (1024, q_width + 256))
+    qd_cp = []
+    for k, (lo, hi) in enumerate(q_parts):
         part = dot(h_v[...], wq_v[:, lo:hi]).astype(BF16)
         for d in range(8):
             qp[d % 2, d // 2, :, lo:hi] = part[16 * d:16 * d + 16]
-    qd_cp = remote(qp.at[1 - core], qd, qd_ssem, qd_rsem, row, partner)
-    qd_cp.start()
+        cols = pl.ds(lo, hi - lo)
+        qd_cp.append(remote(qp.at[1 - core, :, :, cols], qd.at[:, :, cols], qd_ssem.at[k], qd_rsem.at[k], row, partner))
+        qd_cp[k].start()
 
     def pair_copy(n):
         return remote(dsend.at[n], drecv.at[n], d_ssem.at[n], d_rsem.at[n], row, partner)
@@ -189,15 +194,17 @@
 
     compute_chunk(0)
 
-    qd_cp.wait_recv()
-    qx[...] = (qp[core].astype(F32) + qd[...].astype(F32)).astype(BF16)
     mine = row * 2 + chip
     q_sends = []
-    for s, (dy, dx) in enumerate(((0, 1), (1, 0), (1, 1))):
-        ty, xx = (row + dy) % 2, (chip + dx) % 2
-        cp = remote(qx.at[ty * 2 + xx], qr.at[s], q_ssem.at[s], q_rsem.at[s], ty, xx * 2 + core)
-        cp.start()
-        q_sends.append(cp)
+    for k, (lo, hi) in enumerate(q_parts):
+        qd_cp[k].wait_recv()
+        qx[:, :, lo:hi] = (qp[core, :, :, lo:hi].astype(F32) + qd[:, :, lo:hi].astype(F32)).astype(BF16)
+        for s, (dy, dx) in enumerate(((0, 1), (1, 0), (1, 1))):
+            ty, xx = (row + dy) % 2, (chip + dx) % 2
+            cols = pl.ds(lo, min(hi, q_width) - lo if dy else hi - lo)
+            cp = remote(qx.at[ty * 2 + xx, :, cols], qr.at[s, :, cols], q_ssem.at[k, s], q_rsem.at[k, s], ty, xx * 2 + core)
+            cp.start()
+            q_sends.append(cp)
 
     compute_chunk(1)
 
@@ -228,7 +235,7 @@
     for cp in q_sends:
         cp.wait_recv()
     q_same = qx[mine].astype(F32) + qr[0].astype(F32)
-    q_diff = qr[1].astype(F32) + qr[2].astype(F32)
+    q_diff = qr[1, :, 0:q_width].astype(F32) + qr[2, :, 0:q_width].astype(F32)
     for half, vals in ((row, q_same), (1 - row, q_diff)):
         for head in range(16):
             qscr[half, :, head, :] = rotate(vals[:, 128 * head:128 * head + 128])
@@ -243,7 +250,7 @@
         far_copy(n).wait_send()
     for cp in pre_cp:
         cp.wait()
-    for cp in st_cp + [qd_cp] + q_sends:
+    for cp in st_cp + qd_cp + q_sends:
         cp.wait_send()
 
     def drain(n, carry):
@@ -278,7 +285,7 @@
             VMEM((2, 16, 16, 128), F32),
             VMEM((nc, 2, 2, rows, 256), BF16), VMEM((nc, 2, 2, rows, 256), BF16), VMEM((3, 2, 2, rows, 256), F32),
             VMEM((EARLY, 2, rows, 256), F32), VMEM((EARLY, 2, rows, 256), BF16), VMEM((EARLY, 2, rows, 256), BF16),
-            DMA((3,)), DMA((nc, 2)), DMA((3,)), DMA((3,)), DMA, DMA, DMA((3,)), DMA((3,)), DMA((nc,)), DMA((nc,)), DMA((EARLY,)), DMA((EARLY,)),
+            DMA((3,)), DMA((nc, 2)), DMA((3,)), DMA((3,)), DMA((2,)), DMA((2,)), DMA((2, 3)), DMA((2, 3)), DMA((nc,)), DMA((nc,)), DMA((EARLY,)), DMA((EARLY,)),
         ],
         compiler_params=pltpu.CompilerParams(collective_id=0, has_side_effects=True, vmem_limit_bytes=47 * 2 ** 20),
         name="project",
@@ -426,14 +433,14 @@
 
 
 WIDE = 256 * CHUNKS
-EDGE = 256 * (EARLY + 4)
-ITEMS = ((0, 64, False), (0, 64, True), (64, 96, False), (64, 96, True), (96, 128, False), (96, 128, True))
+EDGE = 256 * (EARLY + 3)
+ITEMS = tuple((32 * r, 32 * r + 32, last) for r in range(4) for last in (False, True))
 
 
 def output_kernel(att_ref, keep_v, pay_v, got_v, x_h, wo_h, wd_h, y_out,
                   x_ref, act_v, in_sem, wo_v, wd_v, attf, acc, ysend, yrecv,
                   wo_sem, wd_sem, a_ssem, a_rsem, f_ssem, f_rsem, g_ssem, g_rsem, h_ssem, h_rsem, c_ssem, c_rsem, y_ssem, y_rsem):
-    greet()
+    greet(MET_LATE)
     row, col, chip, core = here()
     partner = col + 1 - 2 * core
     far = (col + 2) % 4
@@ -447,7 +454,7 @@
 
     for cp in (wd_cp[0], wd_cp[1], wo_cp, wd_cp[2], wd_cp[3]):
         cp.start()
-    greeted()
+    greeted(MET_LATE)
     mine = row * 2 + chip
     around = ((0, 1), (1, 0), (1, 1))
     a_cp = []
@@ -468,7 +475,7 @@
     g_cp, h_cp = [], []
     for item, (lo, hi, last) in enumerate(ITEMS):
         rows = slice(lo, hi)
-        for n in range(4, LATE) if last else range(4):
+        for n in range(3, LATE) if last else range(3):
             g = keep_v[n, 0, rows].astype(F32) + got_v[2 * n, rows].astype(F32)
             u = keep_v[n, 1, rows].astype(F32) + got_v[2 * n + 1, rows].astype(F32)
             at = 256 * (EARLY + n)
@@ -505,16 +512,18 @@
         wo_cp.wait()
         for cp in f_cp + [f_own]:
             cp.wait_recv()
-        acc[...] += dot(attf[...].reshape(128, 2048), wo_v[...])
         wd_cp[2].wait()
         wd_cp[3].wait()
+        every_row = slice(0, 128)
+        early = down(every_row, 2, 0, 256 * EARLY) + down(every_row, 3, 0, 256 * EARLY)
+        acc[...] += dot(attf[...].reshape(128, 2048), wo_v[...]) + early
 
     y_cp = []
 
     def finish(item):
         lo, hi, last = ITEMS[item]
         rows, window = slice(lo, hi), pl.ds(lo, hi - lo)
-        k0, k1 = (EDGE, WIDE) if last else (0, EDGE)
+        k0, k1 = (EDGE, WIDE) if last else (256 * EARLY, EDGE)
         h_cp[item].wait_recv()
         part = acc[rows] + (down(rows, 2, k0, k1) + down(rows, 3, k0, k1))
         if last:

time: 65.5 us -> 63.8 us (0.974)
  Pallas kernels: 61.4 us -> 60 us
    pallas_call x1, Pallas kernels: 21 us -> 20.2 us  [output(): pl.pallas_call(output_kernel, out_shape=pltpu.VMEM((rows, width), BF16),...]
  transfers between devices with their start and end apart: 1 -> 1, of which waited for: 1 -> 1; matrix products, arithmetic and copies ran while one was open for 0% -> 0% of each run, Pallas kernels for 30% -> 31%
where the time goes in v5:
time: 63.8 us; the launch traced here: 63.7 us
  Pallas kernels  60 us (94%)
  waiting for transfers between devices  1.72 us (3%)
  local copies, waits for them, and re-layouts  0.71 us (1%)
  between operations  0.66 us (1%)
    pallas_call x1, Pallas kernels, project(): pl.pallas_call(project_kernel, out_shape=(VMEM((2, 16, 16, 128), BF16), V...  20.4 us
    pallas_call x1, Pallas kernels, output(): pl.pallas_call(output_kernel, out_shape=pltpu.VMEM((rows, width), BF16),...  20.2 us
    pallas_call x1, Pallas kernels, attend(): pl.pallas_call(attend_kernel, out_shape=(jax.ShapeDtypeStruct(k_blk.shape...  19.5 us
    ppermute x1, waiting for transfers between devices, layer_shard(): got = lax.ppermute(pay, 'tx', across)  1.72 us
  transfers between devices with their start and end apart: 1, of which 1 were waited for; matrix products, arithmetic and copies ran while one was open for 0% of the time, Pallas kernels for 31%

profile of v5, /device:TPU:0, one launch (start us, length us, event | category | flops | bytes accessed | tf_op | source)
XLA Modules:
  0.0 63.7 jit_solution(1523498578626648582)
XLA Ops:
  0.6 20.4 %project.1 = (bf16[2,16,16,128]{3,2,1,0:T(8,128)(2,1)S(1)}, f32[2,16,128]{2,1,0:T(8,128)S(1)}, bf16[6,2,128,256]{3,2,1,0:T(8,128)(2,1)S(1)}, bf16[14,128,256]{2,...) custom-call(s32[128]{0:T(128)} %lens_h.3, bf16[128,1024]{1,0:T(8,128)(2,1)} %x_h.3, f32[1,1024]{1,0:T(1,128)} %bitcast.3, ...), custom_call_target="tpu_custom_call" | custom-call | tf_op jit(solution)/shard_map/project/pallas_call | solution.py:268
  21.0 0.6 collective-permute-start
  21.6 19.5 %attend.1 = (bf16[16,4096,128]{2,1,0:T(8,128)(2,1)}, bf16[16,4096,128]{2,1,0:T(8,128)(2,1)}, bf16[2,16,2048]{2,1,0:T(8,128)(2,1)S(1)}) custom-call(s32[128]{0:T(128)} %lens_h.3, bf16[2,16,16,128]{3,2,1,0:T(8,128)(2,1)S(1)} %get-tuple-element.11.q_ref, f32[2,16,128]{2,1,0:T(8,128)S(1)} %get-tuple-element.12.kv_ref, ...), custom_call_target="tpu_custom_call" | custom-call | flops 1073741824 | bytes 67108864 | tf_op jit(solution)/shard_map/attend/pallas_call | solution.py:415
  41.1 1.7 %collective-permute-done.got_v = bf16[14,128,256]{2,1,0:T(8,128)(2,1)S(1)} collective-permute-done((bf16[14,128,256]{2,1,0:T(8,128)(2,1)S(1)}, bf16[14,128,256]{2,1,0:T(8,128)(2,1)S(1)}, u32[]{:S(2)}, u32[]{:S(2)}) %collective-permute-start) | collective-permute-done | bytes 917536 | tf_op jit(solution)/shard_map/ppermute | solution.py:583
  42.8 20.2 %output.1 = bf16[128,1024]{1,0:T(8,128)(2,1)S(1)} custom-call(bf16[2,16,2048]{2,1,0:T(8,128)(2,1)S(1)} %get-tuple-element.14.att_ref, bf16[6,2,128,256]{3,2,1,0:T(8,128)(2,1)S(1)} %get-tuple-element.15.keep_v, bf16[14,128,256]{2,1,0:T(8,128)(2,1)S(1)} %get-tuple-element.16.pay_v, bf16[14,128,256]{2,1,0:T(8,128)(2,1)S(1)} %collective-permute-done.got_v, ...), custom_call_target="tpu_custom_call" | custom-call | tf_op jit(solution)/shard_map/output/pallas_call | solution.py:559
  63.0 0.7 %copy.17 = bf16[128,1024]{1,0:T(8,128)(2,1)} copy(bf16[128,1024]{1,0:T(8,128)(2,1)S(1)} %output.1) | data formatting | bytes 524288
Async XLA Ops:
  21.0 21.8 %collective-permute-start = (bf16[14,128,256]{2,1,0:T(8,128)(2,1)S(1)}, bf16[14,128,256]{2,1,0:T(8,128)(2,1)S(1)}, u32[]{:S(2)}, u32[]{:S(2)}) collective-permute-start(bf16[14,128,256]{2,1,0:T(8,128)(2,1)S(1)} %get-tuple-element.16.pay_v), channel_id=1, source_target_pairs={{0,2},{1,3},{2,0},{3,1},{4,6},{5,7},{6,4},{7,5}} | collective-permute-start | bytes 2752520 | tf_op jit(solution)/shard_map/ppermute | solution.py:583

commit v6 on v5

--- a/solution.py
+++ b/solution.py
@@ -434,7 +434,7 @@
 
 WIDE = 256 * CHUNKS
 EDGE = 256 * (EARLY + 3)
-ITEMS = tuple((32 * r, 32 * r + 32, last) for r in range(4) for last in (False, True))
+ITEMS = tuple((lo, hi, last) for lo, hi in ((0, 48), (48, 80), (80, 112), (112, 128)) for last in (False, True))
 
 
 def output_kernel(att_ref, keep_v, pay_v, got_v, x_h, wo_h, wd_h, y_out,

time: 63.8 us -> 63.7 us (level)
  no operation moved by 1% of the time
where the time goes in v6:
time: 63.7 us; the launch traced here: 63.6 us
  Pallas kernels  60 us (94%)
  waiting for transfers between devices  1.72 us (3%)
  local copies, waits for them, and re-layouts  0.71 us (1%)
  between operations  0.66 us (1%)
    pallas_call x1, Pallas kernels, project(): pl.pallas_call(project_kernel, out_shape=(VMEM((2, 16, 16, 128), BF16), V...  20.4 us
    pallas_call x1, Pallas kernels, output(): pl.pallas_call(output_kernel, out_shape=pltpu.VMEM((rows, width), BF16),...  20.1 us
    pallas_call x1, Pallas kernels, attend(): pl.pallas_call(attend_kernel, out_shape=(jax.ShapeDtypeStruct(k_blk.shape...  19.5 us
    ppermute x1, waiting for transfers between devices, layer_shard(): got = lax.ppermute(pay, 'tx', across)  1.72 us
  transfers between devices with their start and end apart: 1, of which 1 were waited for; matrix products, arithmetic and copies ran while one was open for 0% of the time, Pallas kernels for 31%

profile of v6, /device:TPU:0, one launch (start us, length us, event | category | flops | bytes accessed | tf_op | source)
XLA Modules:
  0.0 63.6 jit_solution(7209254055505621577)
XLA Ops:
  0.6 20.4 %project.1 = (bf16[2,16,16,128]{3,2,1,0:T(8,128)(2,1)S(1)}, f32[2,16,128]{2,1,0:T(8,128)S(1)}, bf16[6,2,128,256]{3,2,1,0:T(8,128)(2,1)S(1)}, bf16[14,128,256]{2,...) custom-call(s32[128]{0:T(128)} %lens_h.3, bf16[128,1024]{1,0:T(8,128)(2,1)} %x_h.3, f32[1,1024]{1,0:T(1,128)} %bitcast.3, ...), custom_call_target="tpu_custom_call" | custom-call | tf_op jit(solution)/shard_map/project/pallas_call | solution.py:268
  21.0 0.6 collective-permute-start
  21.6 19.5 %attend.1 = (bf16[16,4096,128]{2,1,0:T(8,128)(2,1)}, bf16[16,4096,128]{2,1,0:T(8,128)(2,1)}, bf16[2,16,2048]{2,1,0:T(8,128)(2,1)S(1)}) custom-call(s32[128]{0:T(128)} %lens_h.3, bf16[2,16,16,128]{3,2,1,0:T(8,128)(2,1)S(1)} %get-tuple-element.11.q_ref, f32[2,16,128]{2,1,0:T(8,128)S(1)} %get-tuple-element.12.kv_ref, ...), custom_call_target="tpu_custom_call" | custom-call | flops 1073741824 | bytes 67108864 | tf_op jit(solution)/shard_map/attend/pallas_call | solution.py:415
  41.1 1.7 %collective-permute-done.got_v = bf16[14,128,256]{2,1,0:T(8,128)(2,1)S(1)} collective-permute-done((bf16[14,128,256]{2,1,0:T(8,128)(2,1)S(1)}, bf16[14,128,256]{2,1,0:T(8,128)(2,1)S(1)}, u32[]{:S(2)}, u32[]{:S(2)}) %collective-permute-start) | collective-permute-done | bytes 917536 | tf_op jit(solution)/shard_map/ppermute | solution.py:583
  42.8 20.1 %output.1 = bf16[128,1024]{1,0:T(8,128)(2,1)S(1)} custom-call(bf16[2,16,2048]{2,1,0:T(8,128)(2,1)S(1)} %get-tuple-element.14.att_ref, bf16[6,2,128,256]{3,2,1,0:T(8,128)(2,1)S(1)} %get-tuple-element.15.keep_v, bf16[14,128,256]{2,1,0:T(8,128)(2,1)S(1)} %get-tuple-element.16.pay_v, bf16[14,128,256]{2,1,0:T(8,128)(2,1)S(1)} %collective-permute-done.got_v, ...), custom_call_target="tpu_custom_call" | custom-call | tf_op jit(solution)/shard_map/output/pallas_call | solution.py:559
  62.9 0.7 %copy.17 = bf16[128,1024]{1,0:T(8,128)(2,1)} copy(bf16[128,1024]{1,0:T(8,128)(2,1)S(1)} %output.1) | data formatting | bytes 524288
Async XLA Ops:
  21.0 21.8 %collective-permute-start = (bf16[14,128,256]{2,1,0:T(8,128)(2,1)S(1)}, bf16[14,128,256]{2,1,0:T(8,128)(2,1)S(1)}, u32[]{:S(2)}, u32[]{:S(2)}) collective-permute-start(bf16[14,128,256]{2,1,0:T(8,128)(2,1)S(1)} %get-tuple-element.16.pay_v), channel_id=1, source_target_pairs={{0,2},{1,3},{2,0},{3,1},{4,6},{5,7},{6,4},{7,5}} | collective-permute-start | bytes 2752520 | tf_op jit(solution)/shard_map/ppermute | solution.py:583

commit v7 on v6

--- a/solution.py
+++ b/solution.py
@@ -434,7 +434,7 @@
 
 WIDE = 256 * CHUNKS
 EDGE = 256 * (EARLY + 3)
-ITEMS = tuple((lo, hi, last) for lo, hi in ((0, 48), (48, 80), (80, 112), (112, 128)) for last in (False, True))
+ITEMS = tuple((lo, hi, last) for lo, hi in ((0, 48), (48, 96), (96, 112), (112, 128)) for last in (False, True))
 
 
 def output_kernel(att_ref, keep_v, pay_v, got_v, x_h, wo_h, wd_h, y_out,

time: 63.7 us -> 64.1 us (level)
  transfers between devices with their start and end apart: 1 -> 1, of which waited for: 1 -> 1; matrix products, arithmetic and copies ran while one was open for 0% -> 0% of each run, Pallas kernels for 31% -> 30%
where the time goes in v7:
time: 64.1 us; the launch traced here: 64 us
  Pallas kernels  60.2 us (94%)
  waiting for transfers between devices  1.81 us (3%)
  local copies, waits for them, and re-layouts  0.71 us (1%)
  between operations  0.66 us (1%)
    pallas_call x1, Pallas kernels, output(): pl.pallas_call(output_kernel, out_shape=pltpu.VMEM((rows, width), BF16),...  20.4 us
    pallas_call x1, Pallas kernels, project(): pl.pallas_call(project_kernel, out_shape=(VMEM((2, 16, 16, 128), BF16), V...  20.4 us
    pallas_call x1, Pallas kernels, attend(): pl.pallas_call(attend_kernel, out_shape=(jax.ShapeDtypeStruct(k_blk.shape...  19.4 us
    ppermute x1, waiting for transfers between devices, layer_shard(): got = lax.ppermute(pay, 'tx', across)  1.81 us
  transfers between devices with their start and end apart: 1, of which 1 were waited for; matrix products, arithmetic and copies ran while one was open for 0% of the time, Pallas kernels for 30%

profile of v7, /device:TPU:0, one launch (start us, length us, event | category | flops | bytes accessed | tf_op | source)
XLA Modules:
  0.0 64.0 jit_solution(5577951188107296721)
XLA Ops:
  0.6 20.4 %project.1 = (bf16[2,16,16,128]{3,2,1,0:T(8,128)(2,1)S(1)}, f32[2,16,128]{2,1,0:T(8,128)S(1)}, bf16[6,2,128,256]{3,2,1,0:T(8,128)(2,1)S(1)}, bf16[14,128,256]{2,...) custom-call(s32[128]{0:T(128)} %lens_h.3, bf16[128,1024]{1,0:T(8,128)(2,1)} %x_h.3, f32[1,1024]{1,0:T(1,128)} %bitcast.3, ...), custom_call_target="tpu_custom_call" | custom-call | tf_op jit(solution)/shard_map/project/pallas_call | solution.py:268
  21.0 0.6 collective-permute-start
  21.6 19.4 %attend.1 = (bf16[16,4096,128]{2,1,0:T(8,128)(2,1)}, bf16[16,4096,128]{2,1,0:T(8,128)(2,1)}, bf16[2,16,2048]{2,1,0:T(8,128)(2,1)S(1)}) custom-call(s32[128]{0:T(128)} %lens_h.3, bf16[2,16,16,128]{3,2,1,0:T(8,128)(2,1)S(1)} %get-tuple-element.11.q_ref, f32[2,16,128]{2,1,0:T(8,128)S(1)} %get-tuple-element.12.kv_ref, ...), custom_call_target="tpu_custom_call" | custom-call | flops 1073741824 | bytes 67108864 | tf_op jit(solution)/shard_map/attend/pallas_call | solution.py:415
  41.0 1.8 %collective-permute-done.got_v = bf16[14,128,256]{2,1,0:T(8,128)(2,1)S(1)} collective-permute-done((bf16[14,128,256]{2,1,0:T(8,128)(2,1)S(1)}, bf16[14,128,256]{2,1,0:T(8,128)(2,1)S(1)}, u32[]{:S(2)}, u32[]{:S(2)}) %collective-permute-start) | collective-permute-done | bytes 917536 | tf_op jit(solution)/shard_map/ppermute | solution.py:583
  42.8 20.4 %output.1 = bf16[128,1024]{1,0:T(8,128)(2,1)S(1)} custom-call(bf16[2,16,2048]{2,1,0:T(8,128)(2,1)S(1)} %get-tuple-element.14.att_ref, bf16[6,2,128,256]{3,2,1,0:T(8,128)(2,1)S(1)} %get-tuple-element.15.keep_v, bf16[14,128,256]{2,1,0:T(8,128)(2,1)S(1)} %get-tuple-element.16.pay_v, bf16[14,128,256]{2,1,0:T(8,128)(2,1)S(1)} %collective-permute-done.got_v, ...), custom_call_target="tpu_custom_call" | custom-call | tf_op jit(solution)/shard_map/output/pallas_call | solution.py:559
  63.3 0.7 %copy.17 = bf16[128,1024]{1,0:T(8,128)(2,1)} copy(bf16[128,1024]{1,0:T(8,128)(2,1)S(1)} %output.1) | data formatting | bytes 524288
Async XLA Ops:
  21.0 21.8 %collective-permute-start = (bf16[14,128,256]{2,1,0:T(8,128)(2,1)S(1)}, bf16[14,128,256]{2,1,0:T(8,128)(2,1)S(1)}, u32[]{:S(2)}, u32[]{:S(2)}) collective-permute-start(bf16[14,128,256]{2,1,0:T(8,128)(2,1)S(1)} %get-tuple-element.16.pay_v), channel_id=1, source_target_pairs={{0,2},{1,3},{2,0},{3,1},{4,6},{5,7},{6,4},{7,5}} | collective-permute-start | bytes 2752520 | tf_op jit(solution)/shard_map/ppermute | solution.py:583
